TPU v7x, 32 devices: a whole 2x2x4 slice. The times are simulated.
32 devices in a mesh: bx: 4 (over y, x), by: 8 (over z, core).
Axes of the slice: x: 2, y: 2, z: 4, core: 2. Of those that a mesh axis runs over, the one named last changes fastest.
Arguments:
- forcing: float32 [1216, 1024], P('by', 'bx'), may hold values from -20 to 20
- guess: float32 [1216, 1024], P('by', 'bx'), may hold values from -3 to 3
- shift: float32 [1216, 1024], P('by', 'bx'), may hold values from 0.05 to 2
- ocean_mask: int32 [1216, 1024], P('by', 'bx'), may hold values 0 or 1
Outputs:
- solution_field: float32 [1216, 1024], P('by', 'bx')
- residual: float32 [1216, 1024], P('by', 'bx')
- residual_norm: float32 [], replicated
All inputs are finite; a program needn't handle non-finite values. No bound on the sum of `ocean_mask` on one device may be relied on, other than what follows from the above.
Results may differ from a plain program's by a relative error of at most 0.00002.
Values sent between devices are 32-bit elements; how exact they have to be, the bound alone decides.
No kernel may reach another device: no remote copies, remote signals or barrier semaphores. Data moves between devices by JAX's collectives and lax.ppermute only.
A program may use at most 64 MiB of HBM per device.

v0:
```python
import jax
import jax.numpy as jnp
from jax import lax
from jax.sharding import PartitionSpec as P

ITERS = 4


LOW_BOUND = 0.05
HIGH_BOUND = 14.5


def padded_2(block, sides, width):
    for axis, dim in sides:
        count = lax.axis_size(axis)
        forward = [(i, i + 1) for i in range(count - 1)]
        forward.append((count - 1, 0))
        backward = [(target, source) for source, target in forward]
        low = lax.ppermute(
            lax.slice_in_dim(block, block.shape[dim] - width, None, axis=dim), axis, forward
        )
        high = lax.ppermute(lax.slice_in_dim(block, 0, width, axis=dim), axis, backward)
        block = jnp.concatenate([low, block, high], axis=dim)
    return block


def stencil_padded(padded, shift, mask_f):
    center = padded[1:-1, 1:-1]
    sides = padded[2:, 1:-1] + padded[:-2, 1:-1] + padded[1:-1, 2:] + padded[1:-1, :-2]
    corners = padded[2:, 2:] + padded[2:, :-2] + padded[:-2, 2:] + padded[:-2, :-2]
    return mask_f * ((6.0 + shift) * center - sides - 0.5 * corners)


def crop_cycle(values, cycle):
    return values[cycle : values.shape[0] - cycle, cycle : values.shape[1] - cycle]


def local_stencil(values, shift_full, mask_full):
    cycle = (shift_full.shape[0] - values.shape[0]) // 2 + 1
    return stencil_padded(values, crop_cycle(shift_full, cycle), crop_cycle(mask_full, cycle))


def deep_inputs(forcing, guess, shift, mask_f):
    rows, cols = forcing.shape
    depth = ITERS + 1
    stacked = jnp.stack([forcing, guess, shift, mask_f])
    padded = padded_2(stacked, (("bx", 2), ("by", 1)), depth)
    top_rows = stacked[:, rows - depth :, :]
    whole_top = lax.all_gather(top_rows, "bx", axis=2, tiled=True)
    flipped = whole_top[:, ::-1, ::-1]
    extended = jnp.concatenate([flipped[:, :, -depth:], flipped, flipped[:, :, :depth]], axis=2)
    ghost = lax.dynamic_slice_in_dim(extended, lax.axis_index("bx") * cols, cols + 2 * depth, 2)
    row_index = lax.axis_index("by")
    upper_rows = jnp.where(row_index == lax.axis_size("by") - 1, ghost, padded[:, rows + depth :])
    lower_rows = jnp.where(row_index == 0, jnp.zeros_like(ghost), padded[:, :depth])
    return jnp.concatenate([lower_rows, padded[:, depth : rows + depth], upper_rows], axis=1)


def pair_add(first, second):
    total = first[0] + second[0]
    backed = total - first[0]
    error = first[0] - (total - backed) + (second[0] - backed)
    error = error + first[1] + second[1]
    upper = total + error
    lower = error - (upper - total)
    return (upper, lower)


def tree_total(uppers, lowers):
    while uppers.shape[0] > 1:
        if uppers.shape[0] % 2 == 1:
            uppers = jnp.concatenate([uppers, jnp.zeros((1,), uppers.dtype)])
            lowers = jnp.concatenate([lowers, jnp.zeros((1,), lowers.dtype)])
        uppers, lowers = pair_add((uppers[0::2], lowers[0::2]), (uppers[1::2], lowers[1::2]))
    return (uppers[0], lowers[0])


def per_device(forcing, guess, shift, ocean_mask):
    mask_f = ocean_mask.astype(jnp.float32)
    theta = (HIGH_BOUND + LOW_BOUND) / 2.0
    delta = (HIGH_BOUND - LOW_BOUND) / 2.0
    sigma = theta / delta
    rho = 1.0 / sigma
    full = deep_inputs(forcing, guess, shift, mask_f)
    forcing_full = full[0]
    guess_full = full[1]
    shift_full = full[2]
    mask_full = full[3]
    iterate = mask_full * guess_full
    resid = crop_cycle(mask_full * forcing_full, 1) - local_stencil(iterate, shift_full, mask_full)
    direction = resid / theta
    iterate = crop_cycle(iterate, 1)
    for sweep in range(ITERS):
        iterate = iterate + direction
        image = local_stencil(direction, shift_full, mask_full)
        resid = crop_cycle(resid, 1) - image
        rho_next = 1.0 / (2.0 * sigma - rho)
        direction = rho_next * rho * crop_cycle(direction, 1) + 2.0 * rho_next / delta * resid
        rho = rho_next
        iterate = crop_cycle(iterate, 1)
    row_sums = jnp.sum(resid * resid, axis=1)
    upper, lower = tree_total(row_sums, jnp.zeros_like(row_sums))
    all_upper, all_lower = (
        lax.all_gather(upper[None], ("bx", "by"), axis=0, tiled=True),
        lax.all_gather(lower[None], ("bx", "by"), axis=0, tiled=True),
    )
    upper, lower = tree_total(all_upper, all_lower)
    grid_cells = resid.shape[0] * lax.axis_size("by") * resid.shape[1] * lax.axis_size("bx")
    norm_value = jnp.sqrt((upper + lower) / grid_cells)
    return (iterate, resid, norm_value)


def solution(mesh):
    in_specs = (P("by", "bx"), P("by", "bx"), P("by", "bx"), P("by", "bx"))
    out_specs = (P("by", "bx"), P("by", "bx"), P())
    return jax.shard_map(
        per_device, mesh=mesh, in_specs=in_specs, out_specs=out_specs, check_vma=False
    )
```

profile of v0, /device:TPU:0, one launch (start us, length us, event | category | flops | bytes accessed | tf_op | source)
XLA Modules:
  0.0 87.8 jit_solution(3005025311582672974)
XLA Ops:
  0.7 1.0 %convert_bitcast_fusion = f32[1,152,256]{2,1,0:T(8,128)S(1)} fusion(s32[152,256]{1,0:T(8,128)} %param.7), kind=kLoop, calls=%fused_computation.81 | loop fusion | flops 38912 | bytes 311296 | tf_op jit(solution)/shard_map/stack | solution.py:46
  1.7 1.0 %pad_maximum_fusion.1 = f32[4,152,256]{2,1,0:T(8,128)S(1)} fusion(f32[1,152,256]{2,1,0:T(8,128)S(1)} %convert_bitcast_fusion, f32[1,152,256]{2,1,0:T(8,128)S(1)} %bitcast.18, f32[1,152,256]{2,1,0:T(8,128)S(1)} %bitcast.22, f32[1,152,256]{2,1,0:T(8,128)} %bitcast.26), kind=kLoop, calls=%fused_computation.1 | loop fusion | flops 466944 | bytes 1245184 | tf_op jit(solution)/shard_map/stack | solution.py:46
  2.7 0.1 fusion.38
  2.8 3.0 %collective-permute-start = (f32[4,152,5]{2,1,0:T(8,128)S(1)}, f32[4,152,5]{2,1,0:T(8,128)S(1)}, u32[]{:S(2)}, u32[]{:S(2)}) collective-permute-start(f32[4,152,5]{2,1,0:T(8,128)S(1)} %get-tuple-element.62), channel_id=1, source_target_pairs={{0,8},{8,16},{16,24},{24,0},{1,9},{9,17},{17,25},{25,1},{2,10},{10... | collective-permute-start | bytes 36488 | tf_op jit(solution)/shard_map/ppermute | solution.py:19
  5.8 1.0 %collective-permute-start.1 = (f32[4,152,5]{2,1,0:T(8,128)S(1)}, f32[4,152,5]{2,1,0:T(8,128)S(1)}, u32[]{:S(2)}, u32[]{:S(2)}) collective-permute-start(f32[4,152,5]{2,1,0:T(8,128)S(1)} %get-tuple-element.63), channel_id=1, source_target_pairs={{8,0},{16,8},{24,16},{0,24},{9,1},{17,9},{25,17},{1,25},{10,2},{18... | collective-permute-start | bytes 36488 | tf_op jit(solution)/shard_map/ppermute | solution.py:22
  6.9 17.0 %all_gather.9 = f32[4,5,1024]{2,1,0:T(8,128)S(1)} all-gather(f32[4,5,256]{2,1,0:T(8,128)S(1)} %pad_maximum_fusion.8), channel_id=1, replica_groups=mesh['bx'=4,'by'=8] {'bx'}, dimensions={2}, use_global_device_ids=true | all-gather | bytes 102400 | tf_op jit(solution)/shard_map/all_gather | solution.py:49
  24.1 0.7 rev.3
  25.0 0.1 concatenate.28
  25.1 3.6 %collective-permute-start.3 = (f32[4,5,266]{2,1,0:T(8,128)S(1)}, f32[4,5,266]{2,1,0:T(8,128)S(1)}, u32[]{:S(2)}, u32[]{:S(2)}) collective-permute-start(f32[4,5,266]{2,1,0:T(8,128)S(1)} %get-tuple-element.58), channel_id=1, source_target_pairs={{1,0},{2,1},{3,2},{4,3},{5,4},{6,5},{7,6},{0,7},{9,8},{10,9},{11,1... | collective-permute-start | bytes 63848 | tf_op jit(solution)/shard_map/ppermute | solution.py:22
  28.7 0.6 collective-permute-done.2
  29.3 1.1 %collective-permute-done.3 = f32[4,5,266]{2,1,0:T(8,128)S(1)} collective-permute-done((f32[4,5,266]{2,1,0:T(8,128)S(1)}, f32[4,5,266]{2,1,0:T(8,128)S(1)}, u32[]{:S(2)}, u32[]{:S(2)}) %collective-permute-start.3) | collective-permute-done | bytes 21312 | tf_op jit(solution)/shard_map/ppermute | solution.py:22
  30.5 0.4 pad_maximum_fusion
  31.1 0.1 slice.570
  31.2 0.7 broadcast_multiply_fusion
  31.9 0.1 slice.571
  32.0 0.6 multiply_add_fusion.2
  32.6 0.1 slice.572
  32.8 0.6 multiply_add_fusion.1
  33.4 0.6 multiply_add_fusion
  34.1 1.4 %multiply_reduce_fusion = (f32[152]{0:T(256)S(1)}, f32[152,256]{1,0:T(8,128)}, f32[152,256]{1,0:T(8,128)}) fusion(f32[154,258]{1,0:T(8,128)S(1)} %get-tuple-element.49, f32[162,266]{1,0:T(8,128)S(1)} %get-tuple-element.60, f32[162,266]{1,0:T(8,128)S(1)} %get-tuple-element.59, f32[154,258]{1,0:T(8,128)S(1)} %get-tuple-element.50, ...), kind=kLoop, calls=%fused_computation.80 | loop fusion | flops 739176 | bytes 2802272 | tf_op jit(solution)/shard_map/reduce_sum | solution.py:101
  35.5 0.2 slice.471
  35.6 0.2 slice.470
  35.8 0.1 slice.475
  36.0 0.1 slice.474
  36.1 0.1 slice.473
  36.2 0.1 slice.472
  36.6 0.1 slice.477
  38.9 0.6 add_dynamic-update-slice_fusion
  39.5 0.8 subtract_dynamic-update-slice_fusion
  40.3 38.8 %all-reduce.2 = (f32[32]{0:T(128)S(1)}, f32[32]{0:T(128)S(1)}) all-reduce(f32[32]{0:T(128)S(1)} %get-tuple-element.72, f32[32]{0:T(128)S(1)} %subtract_dynamic-update-slice_fusion), channel_id=1, replica_groups=mesh['bx'=4,'by'=8] {'bx','by'}, use_global_device_ids=true, to_apply=%add | all-reduce | flops 64 | bytes 512
  80.8 0.6 fusion.41
  84.1 0.6 fusion.40
  (82 shorter events, 4.7 us)
Async XLA Ops:
  0.6 1.0 %copy-start = (f32[152,256]{1,0:T(8,128)S(1)}, f32[152,256]{1,0:T(8,128)}, u32[]{:S(2)}) copy-start(f32[152,256]{1,0:T(8,128)} %param.6) | copy-start | bytes 466948
  0.6 1.1 %copy-start.1 = (f32[152,256]{1,0:T(8,128)S(1)}, f32[152,256]{1,0:T(8,128)}, u32[]{:S(2)}) copy-start(f32[152,256]{1,0:T(8,128)} %param.5) | copy-start | bytes 466948
  2.7 4.2 %copy-start.2 = (f32[152,256]{1,0:T(8,128)S(1)}, f32[152,256]{1,0:T(8,128)}, u32[]{:S(2)}) copy-start(f32[152,256]{1,0:T(8,128)} %param.4) | copy-start | bytes 466948
  2.8 21.0 %collective-permute-start = (f32[4,152,5]{2,1,0:T(8,128)S(1)}, f32[4,152,5]{2,1,0:T(8,128)S(1)}, u32[]{:S(2)}, u32[]{:S(2)}) collective-permute-start(f32[4,152,5]{2,1,0:T(8,128)S(1)} %get-tuple-element.62), channel_id=1, source_target_pairs={{0,8},{8,16},{16,24},{24,0},{1,9},{9,17},{17,25},{25,1},{2,10},{10... | collective-permute-start | bytes 36488 | tf_op jit(solution)/shard_map/ppermute | solution.py:19
  5.8 18.0 %collective-permute-start.1 = (f32[4,152,5]{2,1,0:T(8,128)S(1)}, f32[4,152,5]{2,1,0:T(8,128)S(1)}, u32[]{:S(2)}, u32[]{:S(2)}) collective-permute-start(f32[4,152,5]{2,1,0:T(8,128)S(1)} %get-tuple-element.63), channel_id=1, source_target_pairs={{8,0},{16,8},{24,16},{0,24},{9,1},{17,9},{25,17},{1,25},{10,2},{18... | collective-permute-start | bytes 36488 | tf_op jit(solution)/shard_map/ppermute | solution.py:22
  24.0 5.4 %collective-permute-start.2 = (f32[4,5,266]{2,1,0:T(8,128)S(1)}, f32[4,5,266]{2,1,0:T(8,128)S(1)}, u32[]{:S(2)}, u32[]{:S(2)}) collective-permute-start(f32[4,5,266]{2,1,0:T(8,128)S(1)} %get-tuple-element.57), channel_id=1, source_target_pairs={{0,1},{1,2},{2,3},{3,4},{4,5},{5,6},{6,7},{7,0},{8,9},{9,10},{10,1... | collective-permute-start | bytes 63848 | tf_op jit(solution)/shard_map/ppermute | solution.py:19
  25.1 5.3 %collective-permute-start.3 = (f32[4,5,266]{2,1,0:T(8,128)S(1)}, f32[4,5,266]{2,1,0:T(8,128)S(1)}, u32[]{:S(2)}, u32[]{:S(2)}) collective-permute-start(f32[4,5,266]{2,1,0:T(8,128)S(1)} %get-tuple-element.58), channel_id=1, source_target_pairs={{1,0},{2,1},{3,2},{4,3},{5,4},{6,5},{7,6},{0,7},{9,8},{10,9},{11,1... | collective-permute-start | bytes 63848 | tf_op jit(solution)/shard_map/ppermute | solution.py:22
where the time goes:
time: 88.3 us; the launch traced here: 87.8 us
  blocking collectives  55.8 us (63%)
  other arithmetic  8.6 us (10%)
  starting transfers between devices  7.68 us (9%)
  local copies, waits for them, and re-layouts  7.26 us (8%)
  between operations  6.75 us (8%)
  waiting for transfers between devices  1.75 us (2%)
    unnamed x1, blocking collectives  38.8 us
    all_gather x1, blocking collectives, deep_inputs(): whole_top = lax.all_gather(top_rows, 'bx', axis=2, tiled=True)  17 us
    ppermute x2, starting transfers between devices, padded_2(): lax.ppermute(lax.slice_in_dim(block, 0, width, axis=dim), axis, backward)  4.6 us
    ppermute x2, starting transfers between devices, padded_2(): lax.ppermute(lax.slice_in_dim(block, block.shape[dim] - width, None, axis...  3.07 us
    add x3, other arithmetic, per_device(): rho_next * rho * crop_cycle(direction, 1) + 2.0 * rho_next / delta * resid  1.94 us
    another operation x2, other arithmetic, deep_inputs(): stacked = jnp.stack([forcing, guess, shift, mask_f])  1.93 us
    slice x12, local copies, waits for them, and re-layouts, tree_total(): uppers[1::2]  1.78 us
  transfers between devices with their start and end apart: 4, of which 2 were waited for; matrix products, arithmetic and copies ran while one was open for 1% of the time, Pallas kernels for 0%

commit v1 on v0

v1 whole, which is shorter than its diff:
```python
import functools

import jax
import jax.numpy as jnp
from jax import lax
from jax.experimental import pallas as pl
from jax.experimental.pallas import tpu as pltpu
from jax.sharding import PartitionSpec as P

ITERS = 4
LOW_BOUND = 0.05
HIGH_BOUND = 14.5

SUB = 8
LANE = 128
FIELDS = 3
VMEM = pl.BlockSpec(memory_space=pltpu.VMEM)
SMEM = pl.BlockSpec(memory_space=pltpu.SMEM)


def call(kernel, shapes, in_specs, out_specs, scratch=(), flops=100000):
    return pl.pallas_call(
        kernel,
        out_shape=shapes,
        in_specs=in_specs,
        out_specs=out_specs,
        scratch_shapes=scratch,
        cost_estimate=pl.CostEstimate(flops=flops, bytes_accessed=0, transcendentals=0),
    )


def masked_fields(forcing, guess, shift, ocean):
    zero = jnp.zeros_like(forcing)
    sea = ocean > 0
    return (
        jnp.where(sea, guess, zero),
        jnp.where(sea, forcing, zero),
        jnp.where(sea, 6.0 + shift, zero),
    )


def edge_kernel(odd_ref, *refs):
    low = [ref[...] for ref in refs[0:4]]
    top = [ref[...] for ref in refs[4:8]]
    near_ref, far_ref = refs[8:10]
    odd = odd_ref[0] == 1
    low = masked_fields(*low)
    top = masked_fields(*top)
    for f in range(FIELDS):
        rows = slice(f * SUB, (f + 1) * SUB)
        near_ref[rows, :] = jnp.where(odd, low[f], top[f])
        far_ref[rows, :] = jnp.where(odd, top[f], low[f])


def pack_columns(fields):
    rows, cols = fields[0].shape
    lane = lax.broadcasted_iota(jnp.int32, (rows, LANE), 1)
    packed = jnp.zeros((rows, LANE), jnp.float32)
    for f, field in enumerate(fields):
        at = f * SUB
        left = field[:, :LANE]
        left = pltpu.roll(left, at, 1) if at else left
        packed = jnp.where((lane >= at) & (lane < at + SUB), left, packed)
        at = (FIELDS + f) * SUB
        right = pltpu.roll(field[:, cols - LANE :], at + SUB, 1)
        packed = jnp.where((lane >= at) & (lane < at + SUB), right, packed)
    return packed


def block_kernel(forcing_ref, guess_ref, shift_ref, ocean_ref, x_ref, r_ref, c_ref, columns_ref):
    fields = masked_fields(forcing_ref[...], guess_ref[...], shift_ref[...], ocean_ref[...])
    for ref, field in zip((x_ref, r_ref, c_ref), fields):
        ref[...] = field
    packed = pack_columns(fields)
    width = columns_ref.shape[1]
    packed = jnp.concatenate([packed, jnp.zeros((width - packed.shape[0], LANE), jnp.float32)], axis=0)
    columns_ref[...] = packed.T[: 2 * FIELDS * SUB]


def mirrored(tile):
    back = LANE - 1 - lax.broadcasted_iota(jnp.int32, (SUB, LANE), 1)
    up = SUB - 1 - lax.broadcasted_iota(jnp.int32, (SUB, LANE), 0)
    parts = []
    for at in reversed(range(0, tile.shape[1], LANE)):
        part = jnp.take_along_axis(tile[:, at : at + LANE], back, axis=1)
        parts.append(jnp.take_along_axis(part, up, axis=0))
    return jnp.concatenate(parts, axis=1)


def halo_kernel(rows, where_ref, near_ref, far_ref, columns_ref, halo_ref, a_ref, b_ref):
    odd, fold, odd_x = where_ref[0] == 1, where_ref[1] == 1, where_ref[2] == 1
    n = FIELDS * SUB
    near, far = near_ref[...], far_ref[...]
    halo_ref[0:n, :] = jnp.where(odd, far, near)
    halo_ref[n : 2 * n, :] = jnp.where(odd, near, far)

    @pl.when(fold)
    def _():
        for f in range(FIELDS):
            at = slice(f * SUB, (f + 1) * SUB)
            halo_ref[at, :] = mirrored(halo_ref[at, :])

    fields = [
        jnp.concatenate([halo_ref[f * SUB : (f + 1) * SUB, :], halo_ref[n + f * SUB : n + (f + 1) * SUB, :]], axis=0)
        for f in range(FIELDS)
    ]
    packed = pack_columns(fields)
    width = columns_ref.shape[1]
    start = rows // LANE * LANE
    before, after = rows - start, width - rows - 2 * SUB
    pieces = [packed]
    if before:
        pieces.insert(0, jnp.zeros((before, LANE), jnp.float32))
    if after:
        pieces.append(jnp.zeros((after, LANE), jnp.float32))
    ends = jnp.concatenate(pieces, axis=0).T[: 2 * n]
    for at, first, second in ((slice(0, start), None, None), (slice(start, width), ends[:n], ends[n:])):
        if at.stop == at.start:
            continue
        left, right = columns_ref[0:n, at], columns_ref[n : 2 * n, at]
        if first is not None:
            left, right = left + first, right + second
        a_ref[:, at] = jnp.where(odd_x, left, right)
        b_ref[:, at] = jnp.where(odd_x, right, left)


def coefficients():
    theta = (HIGH_BOUND + LOW_BOUND) / 2.0
    delta = (HIGH_BOUND - LOW_BOUND) / 2.0
    sigma = theta / delta
    rho = 1.0 / sigma
    steps = []
    for _ in range(ITERS):
        following = 1.0 / (2.0 * sigma - rho)
        steps.append((following * rho, 2.0 * following / delta))
        rho = following
    return theta, steps


def pair_add(first, second):
    total = first[0] + second[0]
    backed = total - first[0]
    error = first[0] - (total - backed) + (second[0] - backed)
    error = error + first[1] + second[1]
    upper = total + error
    lower = error - (upper - total)
    return (upper, lower)


def pair_tree(pairs):
    while len(pairs) > 1:
        tail = pairs[len(pairs) // 2 * 2 :]
        pairs = [pair_add(pairs[i], pairs[i + 1]) for i in range(0, len(pairs) - 1, 2)] + tail
    return pairs[0]


def pair_total(pairs):
    total = pair_tree(pairs)
    for by in (4, 2, 1):
        total = pair_add(total, tuple(pltpu.roll(v, by, 0) for v in total))
    return total


def sweep_kernel(where_ref, x_ref, f_ref, c_ref, halo_ref, a_ref, b_ref, out_x_ref, out_r_ref, pair_ref, d_s, r_s, c_s):
    odd_x = where_ref[2] == 1
    rows, cols = x_ref.shape
    n = FIELDS * SUB
    tiles, inner = d_s.shape[0] // SUB, rows // SUB
    wide = cols + LANE
    high = d_s.shape[0]
    a, b = a_ref[...], b_ref[...]
    left, right = jnp.where(odd_x, a, b), jnp.where(odd_x, b, a)
    pieces = []
    for f in range(FIELDS):
        at = slice(f * SUB, (f + 1) * SUB)
        pieces += [left[at], right[at]]
    pieces.append(jnp.zeros((LANE - 2 * n, a.shape[1]), jnp.float32))
    sides = jnp.concatenate(pieces, axis=0).T
    for f, (ref, main) in enumerate(((d_s, x_ref), (r_s, f_ref), (c_s, c_ref))):
        at = slice(f * SUB, (f + 1) * SUB)
        ref[0:rows, 0:cols] = main[...]
        ref[rows : rows + SUB, 0:cols] = halo_ref[at, :]
        ref[rows + SUB : high, 0:cols] = halo_ref[n + f * SUB : n + (f + 1) * SUB, :]
        ref[:, cols:wide] = pltpu.roll(sides[0:high], LANE - (2 * f + 1) * SUB, 1)

    theta, steps = coefficients()
    row_id = lax.broadcasted_iota(jnp.int32, (SUB, wide), 0)
    first_row, last_row = row_id == 0, row_id == SUB - 1

    def across(i):
        v = d_s[i * SUB : (i + 1) * SUB, :]
        pair = pltpu.roll(v, 1, 1) + pltpu.roll(v, wide - 1, 1)
        mixed = v + 0.5 * pair
        return v, pair, pltpu.roll(mixed, 1, 0), pltpu.roll(mixed, SUB - 1, 0)

    squares = []
    for sweep in range(ITERS + 1):
        head, tail = across(0), across(tiles - 1)
        before, now = tail, head
        for i in range(tiles):
            if i < tiles - 2:
                after = across(i + 1)
            else:
                after = tail if i == tiles - 2 else head
            v, pair, down, up = now
            from_below = jnp.where(first_row, before[2], down)
            from_above = jnp.where(last_row, after[3], up)
            at = slice(i * SUB, (i + 1) * SUB)
            c = c_s[at, :]
            image = jnp.where(c > 0.0, c * v - (pair + (from_below + from_above)), jnp.zeros_like(c))
            r = r_s[at, :] - image
            if sweep < ITERS:
                r_s[at, :] = r
                if sweep == 0:
                    d = r * (1.0 / theta)
                else:
                    keep, gain = steps[sweep - 1]
                    d = keep * v + gain * r
                d_s[at, :] = d
                if i < inner:
                    old = x_ref[at, :] if sweep == 0 else out_x_ref[at, :]
                    out_x_ref[at, :] = old + d[:, :cols]
            elif i < inner:
                r = r[:, :cols]
                out_r_ref[at, :] = r
                squares.append(jnp.sum(r * r, axis=1, keepdims=True))
            before, now = now, after
    zero = jnp.zeros_like(squares[0])
    upper, lower = pair_total([(q, zero) for q in squares])
    lane = lax.broadcasted_iota(jnp.int32, (SUB, LANE), 1)
    tile = jnp.where(lane < LANE // 2, upper, lower)
    for i in range(pair_ref.shape[0] // SUB):
        pair_ref[i * SUB : (i + 1) * SUB, :] = tile


def norm_kernel(cells, pairs_ref, out_ref):
    pairs = []
    for i in range(pairs_ref.shape[0] // SUB):
        upper = pairs_ref[i * SUB : (i + 1) * SUB, :]
        pairs.append((upper, pltpu.roll(upper, LANE // 2, 1)))
    upper, lower = pair_total(pairs)
    out_ref[0] = jnp.sqrt((upper + lower) * (1.0 / cells))[0, 0]


def swap(value, mesh_shape, partner):
    wide, high = mesh_shape
    moves = []
    for b in range(wide):
        for j in range(high):
            other = partner(b, j)
            if other is not None:
                moves.append((b * high + j, other[0] * high + other[1]))
    return lax.ppermute(value, ("bx", "by"), moves)


def per_device(forcing, guess, shift, ocean):
    rows, cols = forcing.shape
    wide, high = lax.axis_size("bx"), lax.axis_size("by")
    devices = wide * high
    assert rows % SUB == 0 and cols % LANE == 0 and devices % SUB == 0
    assert wide % 2 == 0 and high % 2 == 0
    n = FIELDS * SUB
    tall = rows + 2 * SUB
    span = -(-tall // LANE) * LANE
    f32 = functools.partial(jax.ShapeDtypeStruct, dtype=jnp.float32)
    bx, by = lax.axis_index("bx"), lax.axis_index("by")
    where = jnp.stack([by % 2, (by == high - 1).astype(jnp.int32), bx % 2])

    last = rows // SUB - 1
    fields = (forcing, guess, shift, ocean)
    low_spec = pl.BlockSpec((SUB, cols), lambda i: (0, 0))
    top_spec = pl.BlockSpec((SUB, cols), lambda i: (last, 0))
    full_spec = pl.BlockSpec((n, cols), lambda i: (0, 0))
    near, far = pl.pallas_call(
        edge_kernel,
        grid=(1,),
        out_shape=(f32((n, cols)), f32((n, cols))),
        in_specs=[SMEM] + [low_spec] * 4 + [top_spec] * 4,
        out_specs=(full_spec, full_spec),
    )(where, *fields, *fields)

    def own_chip(b, j):
        return (b, j ^ 1)

    def next_chip(b, j):
        if j == 0:
            return None
        if j == high - 1:
            return (wide - 1 - b, j)
        return (b, ((j - 1) ^ 1) + 1)

    def even_pair(b, j):
        return (b ^ 1, j)

    def odd_pair(b, j):
        return ((((b - 1) % wide) ^ 1) + 1) % wide, j

    shape = (wide, high)
    near = swap(near, shape, own_chip)
    far = swap(far, shape, next_chip)
    x, f, c, columns = call(
        block_kernel,
        (f32((rows, cols)),) * 3 + (f32((2 * n, span)),),
        [VMEM] * 4,
        (VMEM,) * 4,
    )(*fields)
    halo, a, b = call(
        functools.partial(halo_kernel, rows),
        (f32((2 * n, cols)), f32((n, span)), f32((n, span))),
        [SMEM] + [VMEM] * 3,
        (VMEM,) * 3,
    )(where, near, far, columns)
    a = swap(a, shape, even_pair)
    b = swap(b, shape, odd_pair)
    x, r, pairs = call(
        sweep_kernel,
        (f32((rows, cols)), f32((rows, cols)), f32((devices, LANE))),
        [SMEM] + [VMEM] * 6,
        (VMEM,) * 3,
        [pltpu.VMEM((tall, cols + LANE), jnp.float32)] * 3,
    )(where, x, f, c, halo, a, b)
    pairs = lax.all_to_all(pairs, ("bx", "by"), 0, 0, tiled=True)
    cells = rows * cols * devices
    norm = call(functools.partial(norm_kernel, cells), f32((1,)), [VMEM], SMEM)(pairs)
    return (x, r, norm[0])


def solution(mesh):
    spec = P("by", "bx")
    return jax.shard_map(
        per_device, mesh=mesh, in_specs=(spec,) * 4, out_specs=(spec, spec, P()), check_vma=False
    )
```

time: 88.3 us -> 36.4 us (0.41)
  blocking collectives: 55.8 us -> 14.7 us
  Pallas kernels: 0 us -> 10.2 us
  other arithmetic: 8.6 us -> 0.65 us
  local copies, waits for them, and re-layouts: 7.26 us -> 1.19 us
  between operations: 6.75 us -> 0.68 us
  starting transfers between devices: 7.68 us -> 5.11 us
  waiting for transfers between devices: 1.75 us -> 3.45 us
    unnamed x1 -> x0, blocking collectives: 38.8 us -> none
    all_gather x1 -> x0, blocking collectives: 17 us -> none  [deep_inputs(): whole_top = lax.all_gather(top_rows, 'bx', axis=2, tiled=True)]
    all_to_all x0 -> x1, blocking collectives: none -> 14.7 us  [per_device(): pairs = lax.all_to_all(pairs, ('bx', 'by'), 0, 0, tiled=True)]
    pallas_call x0 -> x5, Pallas kernels: none -> 10.2 us  [the longest x1 3.75 us: per_device(): call(sweep_kernel, (f32((rows, cols)), f32((rows, cols)), f32((devices, L...]
    slice x51 -> x0, local copies, waits for them, and re-layouts: 6.32 us -> none  [the longest x12 1.78 us: tree_total(): uppers[1::2]]
    ppermute x4, starting transfers between devices: 7.68 us -> 5.11 us  [swap(): return lax.ppermute(value, ('bx', 'by'), moves)]
    add x14 -> x0, other arithmetic: 2.08 us -> none  [the longest x3 1.94 us: per_device(): rho_next * rho * crop_cycle(direction, 1) + 2.0 * rho_next / delta * resid]
    ppermute x4, waiting for transfers between devices: 1.75 us -> 3.45 us  [swap(): return lax.ppermute(value, ('bx', 'by'), moves)]
  transfers between devices with their start and end apart: 4 -> 4, of which waited for: 2 -> 2; matrix products, arithmetic and copies ran while one was open for 1% -> 0% of each run, Pallas kernels for 0% -> 6%
where the time goes in v1:
time: 36.4 us; the launch traced here: 36 us
  blocking collectives  14.7 us (40%)
  Pallas kernels  10.2 us (28%)
  starting transfers between devices  5.11 us (14%)
  waiting for transfers between devices  3.45 us (9%)
  local copies, waits for them, and re-layouts  1.19 us (3%)
  between operations  0.68 us (2%)
  other arithmetic  0.65 us (2%)
    all_to_all x1, blocking collectives, per_device(): pairs = lax.all_to_all(pairs, ('bx', 'by'), 0, 0, tiled=True)  14.7 us
    ppermute x4, starting transfers between devices, swap(): return lax.ppermute(value, ('bx', 'by'), moves)  5.11 us
    pallas_call x1, Pallas kernels, per_device(): call(sweep_kernel, (f32((rows, cols)), f32((rows, cols)), f32((devices, L...  3.75 us
    ppermute x4, waiting for transfers between devices, swap(): return lax.ppermute(value, ('bx', 'by'), moves)  3.45 us
    pallas_call x1, Pallas kernels, per_device(): call(block_kernel, (f32((rows, cols)),) * 3 + (f32((2 * n, span)),), [VME...  2.02 us
    pallas_call x1, Pallas kernels, per_device(): call(functools.partial(halo_kernel, rows), (f32((2 * n, cols)), f32((n, s...  1.62 us
    pallas_call x1, Pallas kernels, per_device(): pl.pallas_call(edge_kernel, grid=(1,), out_shape=(f32((n, cols)), f32((n,...  1.45 us
    pallas_call x1, Pallas kernels, per_device(): call(functools.partial(norm_kernel, cells), f32((1,)), [VMEM], SMEM)(pairs)  1.39 us
  transfers between devices with their start and end apart: 4, of which 2 were waited for; matrix products, arithmetic and copies ran while one was open for 0% of the time, Pallas kernels for 6%

profile of v1, /device:TPU:0, one launch (start us, length us, event | category | flops | bytes accessed | tf_op | source)
XLA Modules:
  0.0 36.0 jit_solution(1399611359234333034)
XLA Ops:
  0.6 0.7 %pad_add_fusion.odd_ref.where_ref = s32[3]{0:T(128)} fusion(s32[1]{0:T(128)} %bitcast.2, s32[1]{0:T(128)} %bitcast.1, s32[1]{0:T(128)} %bitcast), kind=kLoop, calls=%fused_computation | loop fusion | flops 6 | bytes 24 | tf_op jit(solution)/shard_map/stack | solution.py:267
  1.3 1.4 %shard_map.68 = (f32[24,256]{1,0:T(8,128)}, f32[24,256]{1,0:T(8,128)}) custom-call(s32[3]{0:T(128)} %pad_add_fusion.odd_ref.where_ref, f32[152,256]{1,0:T(8,128)} %refs_4_.1, f32[152,256]{1,0:T(8,128)} %refs_5_.1, f32[152,256]{1,0:T(8,128)} %refs_6_.1, s32[152,256]{1,0:T(8,128)} %refs_7_.1, f32[152,256]{1,0:T(8,128)} %refs_4_.1, f32[152,256]{1,0:T(8,128)} %refs_5_.1, ...), custom_call_target="tpu_custom_call" | custom-call | tf_op jit(solution)/shard_map/pallas_call | solution.py:274
  2.7 0.5 %collective-permute-start = (f32[24,256]{1,0:T(8,128)}, f32[24,256]{1,0:T(8,128)S(1)}, u32[]{:S(2)}, u32[]{:S(2)}) collective-permute-start(f32[24,256]{1,0:T(8,128)} %get-tuple-element.18), channel_id=1, source_target_pairs={{0,1},{1,0},{2,3},{3,2},{4,5},{5,4},{6,7},{7,6},{8,9},{9,8},{10,11... | collective-permute-start | bytes 73736 | tf_op jit(solution)/shard_map/ppermute | solution.py:253
  3.2 0.7 %collective-permute-start.1 = (f32[24,256]{1,0:T(8,128)}, f32[24,256]{1,0:T(8,128)S(1)}, u32[]{:S(2)}, u32[]{:S(2)}) collective-permute-start(f32[24,256]{1,0:T(8,128)} %get-tuple-element.19), channel_id=1, source_target_pairs={{1,2},{2,1},{3,4},{4,3},{5,6},{6,5},{7,31},{9,10},{10,9},{11,12},{... | collective-permute-start | bytes 73736 | tf_op jit(solution)/shard_map/ppermute | solution.py:253
  3.9 2.0 %shard_map.67 = (f32[152,256]{1,0:T(8,128)}, f32[152,256]{1,0:T(8,128)}, f32[152,256]{1,0:T(8,128)}, f32[48,256]{1,0:T(8,128)}) custom-call(f32[152,256]{1,0:T(8,128)} %refs_4_.1, f32[152,256]{1,0:T(8,128)} %refs_5_.1, f32[152,256]{1,0:T(8,128)} %refs_6_.1, s32[152,256]{1,0:T(8,128)} %refs_7_.1), custom_call_target="tpu_custom_call" | custom-call | flops 100000 | tf_op jit(solution)/shard_map/pallas_call | solution.py:301
  5.9 0.0 collective-permute-done.near_ref
  5.9 0.0 copy-start.2
  5.9 0.0 collective-permute-done.1.far_ref
  5.9 0.0 copy-start.3
  5.9 0.6 %copy-done.2 = f32[24,256]{1,0:T(8,128)} copy-done((f32[24,256]{1,0:T(8,128)}, f32[24,256]{1,0:T(8,128)S(1)}, u32[]{:S(2)}) %copy-start.2) | copy-done | bytes 24600
  6.5 0.0 copy-done.3
  6.5 1.6 %shard_map.69 = (f32[48,256]{1,0:T(8,128)}, f32[24,256]{1,0:T(8,128)}, f32[24,256]{1,0:T(8,128)}) custom-call(s32[3]{0:T(128)} %pad_add_fusion.odd_ref.where_ref, f32[24,256]{1,0:T(8,128)} %copy-done.2, f32[24,256]{1,0:T(8,128)} %copy-done.3, f32[48,256]{1,0:T(8,128)} %get-tuple-element.20.columns_ref), custom_call_target="tpu_custom_call" | custom-call | flops 100000 | tf_op jit(solution)/shard_map/pallas_call | solution.py:307
  8.2 2.5 %collective-permute-start.2 = (f32[24,256]{1,0:T(8,128)}, f32[24,256]{1,0:T(8,128)S(1)}, u32[]{:S(2)}, u32[]{:S(2)}) collective-permute-start(f32[24,256]{1,0:T(8,128)} %get-tuple-element.22), channel_id=1, source_target_pairs={{0,8},{1,9},{2,10},{3,11},{4,12},{5,13},{6,14},{7,15},{8,0},{9,1},... | collective-permute-start | bytes 73736 | tf_op jit(solution)/shard_map/ppermute | solution.py:253
  10.6 1.5 %collective-permute-start.3 = (f32[24,256]{1,0:T(8,128)}, f32[24,256]{1,0:T(8,128)S(1)}, u32[]{:S(2)}, u32[]{:S(2)}) collective-permute-start(f32[24,256]{1,0:T(8,128)} %get-tuple-element.23), channel_id=1, source_target_pairs={{0,24},{1,25},{2,26},{3,27},{4,28},{5,29},{6,30},{7,31},{8,16},{9,... | collective-permute-start | bytes 73736 | tf_op jit(solution)/shard_map/ppermute | solution.py:253
  12.1 0.5 %collective-permute-done.2.a_ref = f32[24,256]{1,0:T(8,128)S(1)} collective-permute-done((f32[24,256]{1,0:T(8,128)}, f32[24,256]{1,0:T(8,128)S(1)}, u32[]{:S(2)}, u32[]{:S(2)}) %collective-permute-start.2) | collective-permute-done | bytes 24608 | tf_op jit(solution)/shard_map/ppermute | solution.py:253
  12.7 0.0 copy-start
  12.7 2.9 %collective-permute-done.3.b_ref = f32[24,256]{1,0:T(8,128)S(1)} collective-permute-done((f32[24,256]{1,0:T(8,128)}, f32[24,256]{1,0:T(8,128)S(1)}, u32[]{:S(2)}, u32[]{:S(2)}) %collective-permute-start.3) | collective-permute-done | bytes 24608 | tf_op jit(solution)/shard_map/ppermute | solution.py:253
  15.6 0.0 copy-start.1
  15.6 0.0 copy-done
  15.6 0.6 %copy-done.1 = f32[24,256]{1,0:T(8,128)} copy-done((f32[24,256]{1,0:T(8,128)}, f32[24,256]{1,0:T(8,128)S(1)}, u32[]{:S(2)}) %copy-start.1) | copy-done | bytes 24600
  16.2 3.8 %shard_map.70 = (f32[152,256]{1,0:T(8,128)}, f32[152,256]{1,0:T(8,128)}, f32[32,128]{1,0:T(8,128)}) custom-call(s32[3]{0:T(128)} %pad_add_fusion.odd_ref.where_ref, f32[152,256]{1,0:T(8,128)} %get-tuple-element.15.x_ref, f32[152,256]{1,0:T(8,128)} %get-tuple-element.16.f_ref, f32[152,256]{1,0:T(8,128)} %get-tuple-element.17.c_ref, ...), custom_call_target="tpu_custom_call" | custom-call | flops 100000 | tf_op jit(solution)/shard_map/pallas_call | solution.py:315
  19.9 14.7 %all_to_all.11 = f32[32,1,128]{2,1,0:T(1,128)} all-to-all(f32[32,1,128]{2,1,0:T(1,128)} %bitcast.9), channel_id=1, replica_groups=mesh['bx'=4,'by'=8] {'bx','by'}, dimensions={0} | all-to-all | bytes 32768 | tf_op jit(solution)/shard_map/all_to_all | solution.py:322
  34.6 1.4 %shard_map.71 = f32[1]{0:T(128)} custom-call(f32[32,128]{1,0:T(8,128)} %bitcast.8), custom_call_target="tpu_custom_call" | custom-call | flops 100000 | tf_op jit(solution)/shard_map/pallas_call | solution.py:324
Async XLA Ops:
  2.7 3.2 %collective-permute-start = (f32[24,256]{1,0:T(8,128)}, f32[24,256]{1,0:T(8,128)S(1)}, u32[]{:S(2)}, u32[]{:S(2)}) collective-permute-start(f32[24,256]{1,0:T(8,128)} %get-tuple-element.18), channel_id=1, source_target_pairs={{0,1},{1,0},{2,3},{3,2},{4,5},{5,4},{6,7},{7,6},{8,9},{9,8},{10,11... | collective-permute-start | bytes 73736 | tf_op jit(solution)/shard_map/ppermute | solution.py:253
  3.2 2.7 %collective-permute-start.1 = (f32[24,256]{1,0:T(8,128)}, f32[24,256]{1,0:T(8,128)S(1)}, u32[]{:S(2)}, u32[]{:S(2)}) collective-permute-start(f32[24,256]{1,0:T(8,128)} %get-tuple-element.19), channel_id=1, source_target_pairs={{1,2},{2,1},{3,4},{4,3},{5,6},{6,5},{7,31},{9,10},{10,9},{11,12},{... | collective-permute-start | bytes 73736 | tf_op jit(solution)/shard_map/ppermute | solution.py:253
  5.9 0.6 %copy-start.2 = (f32[24,256]{1,0:T(8,128)}, f32[24,256]{1,0:T(8,128)S(1)}, u32[]{:S(2)}) copy-start(f32[24,256]{1,0:T(8,128)S(1)} %collective-permute-done.near_ref) | copy-start | bytes 73732
  5.9 0.6 %copy-start.3 = (f32[24,256]{1,0:T(8,128)}, f32[24,256]{1,0:T(8,128)S(1)}, u32[]{:S(2)}) copy-start(f32[24,256]{1,0:T(8,128)S(1)} %collective-permute-done.1.far_ref) | copy-start | bytes 73732
  8.2 4.5 %collective-permute-start.2 = (f32[24,256]{1,0:T(8,128)}, f32[24,256]{1,0:T(8,128)S(1)}, u32[]{:S(2)}, u32[]{:S(2)}) collective-permute-start(f32[24,256]{1,0:T(8,128)} %get-tuple-element.22), channel_id=1, source_target_pairs={{0,8},{1,9},{2,10},{3,11},{4,12},{5,13},{6,14},{7,15},{8,0},{9,1},... | collective-permute-start | bytes 73736 | tf_op jit(solution)/shard_map/ppermute | solution.py:253
  10.6 4.9 %collective-permute-start.3 = (f32[24,256]{1,0:T(8,128)}, f32[24,256]{1,0:T(8,128)S(1)}, u32[]{:S(2)}, u32[]{:S(2)}) collective-permute-start(f32[24,256]{1,0:T(8,128)} %get-tuple-element.23), channel_id=1, source_target_pairs={{0,24},{1,25},{2,26},{3,27},{4,28},{5,29},{6,30},{7,31},{8,16},{9,... | collective-permute-start | bytes 73736 | tf_op jit(solution)/shard_map/ppermute | solution.py:253
  12.7 2.9 %copy-start = (f32[24,256]{1,0:T(8,128)}, f32[24,256]{1,0:T(8,128)S(1)}, u32[]{:S(2)}) copy-start(f32[24,256]{1,0:T(8,128)S(1)} %collective-permute-done.2.a_ref) | copy-start | bytes 73732
  15.6 0.6 %copy-start.1 = (f32[24,256]{1,0:T(8,128)}, f32[24,256]{1,0:T(8,128)S(1)}, u32[]{:S(2)}) copy-start(f32[24,256]{1,0:T(8,128)S(1)} %collective-permute-done.3.b_ref) | copy-start | bytes 73732

commit v2 on v1

--- a/solution.py
+++ b/solution.py
@@ -16,6 +16,8 @@
 FIELDS = 3
 VMEM = pl.BlockSpec(memory_space=pltpu.VMEM)
 SMEM = pl.BlockSpec(memory_space=pltpu.SMEM)
+HBM = pl.BlockSpec(memory_space=pltpu.HBM)
+GRANT = pltpu.CompilerParams(vmem_limit_bytes=8 << 20)
 
 
 def call(kernel, shapes, in_specs, out_specs, scratch=(), flops=100000):
@@ -26,6 +28,7 @@
         out_specs=out_specs,
         scratch_shapes=scratch,
         cost_estimate=pl.CostEstimate(flops=flops, bytes_accessed=0, transcendentals=0),
+        compiler_params=GRANT,
     )
 
 
@@ -39,17 +42,30 @@
     )
 
 
-def edge_kernel(odd_ref, *refs):
-    low = [ref[...] for ref in refs[0:4]]
-    top = [ref[...] for ref in refs[4:8]]
-    near_ref, far_ref = refs[8:10]
-    odd = odd_ref[0] == 1
-    low = masked_fields(*low)
-    top = masked_fields(*top)
+def is_odd(axis):
+    return lax.rem(lax.axis_index(axis), 2) == 1
+
+
+def edge_kernel(*refs):
+    near_ref, far_ref = refs[4:6]
+    low_s, top_s = refs[6:10], refs[10:14]
+    sem = refs[14]
+    rows = refs[0].shape[0]
+    copies = []
+    for i in range(4):
+        copies.append(pltpu.make_async_copy(refs[i].at[0:SUB, :], low_s[i], sem.at[2 * i]))
+        copies.append(pltpu.make_async_copy(refs[i].at[rows - SUB : rows, :], top_s[i], sem.at[2 * i + 1]))
+    for copy in copies:
+        copy.start()
+    odd = is_odd("by")
+    for copy in copies:
+        copy.wait()
+    low = masked_fields(*(ref[...] for ref in low_s))
+    top = masked_fields(*(ref[...] for ref in top_s))
     for f in range(FIELDS):
-        rows = slice(f * SUB, (f + 1) * SUB)
-        near_ref[rows, :] = jnp.where(odd, low[f], top[f])
-        far_ref[rows, :] = jnp.where(odd, top[f], low[f])
+        at = slice(f * SUB, (f + 1) * SUB)
+        near_ref[at, :] = jnp.where(odd, low[f], top[f])
+        far_ref[at, :] = jnp.where(odd, top[f], low[f])
 
 
 def pack_columns(fields):
@@ -67,8 +83,15 @@
     return packed
 
 
-def block_kernel(forcing_ref, guess_ref, shift_ref, ocean_ref, x_ref, r_ref, c_ref, columns_ref):
-    fields = masked_fields(forcing_ref[...], guess_ref[...], shift_ref[...], ocean_ref[...])
+def block_kernel(*refs):
+    x_ref, r_ref, c_ref, columns_ref = refs[4:8]
+    held, sem = refs[8:12], refs[12]
+    copies = [pltpu.make_async_copy(refs[i], held[i], sem.at[i]) for i in range(4)]
+    for copy in copies:
+        copy.start()
+    for copy in copies:
+        copy.wait()
+    fields = masked_fields(*(ref[...] for ref in held))
     for ref, field in zip((x_ref, r_ref, c_ref), fields):
         ref[...] = field
     packed = pack_columns(fields)
@@ -87,8 +110,9 @@
     return jnp.concatenate(parts, axis=1)
 
 
-def halo_kernel(rows, where_ref, near_ref, far_ref, columns_ref, halo_ref, a_ref, b_ref):
-    odd, fold, odd_x = where_ref[0] == 1, where_ref[1] == 1, where_ref[2] == 1
+def halo_kernel(rows, near_ref, far_ref, columns_ref, halo_ref, a_ref, b_ref):
+    odd, odd_x = is_odd("by"), is_odd("bx")
+    fold = lax.axis_index("by") == lax.axis_size("by") - 1
     n = FIELDS * SUB
     near, far = near_ref[...], far_ref[...]
     halo_ref[0:n, :] = jnp.where(odd, far, near)
@@ -161,8 +185,8 @@
     return total
 
 
-def sweep_kernel(where_ref, x_ref, f_ref, c_ref, halo_ref, a_ref, b_ref, out_x_ref, out_r_ref, pair_ref, d_s, r_s, c_s):
-    odd_x = where_ref[2] == 1
+def sweep_kernel(x_ref, f_ref, c_ref, halo_ref, a_ref, b_ref, out_x_ref, out_r_ref, pair_ref, d_s, r_s, c_s):
+    odd_x = is_odd("bx")
     rows, cols = x_ref.shape
     n = FIELDS * SUB
     tiles, inner = d_s.shape[0] // SUB, rows // SUB
@@ -263,21 +287,15 @@
     tall = rows + 2 * SUB
     span = -(-tall // LANE) * LANE
     f32 = functools.partial(jax.ShapeDtypeStruct, dtype=jnp.float32)
-    bx, by = lax.axis_index("bx"), lax.axis_index("by")
-    where = jnp.stack([by % 2, (by == high - 1).astype(jnp.int32), bx % 2])
-
-    last = rows // SUB - 1
     fields = (forcing, guess, shift, ocean)
-    low_spec = pl.BlockSpec((SUB, cols), lambda i: (0, 0))
-    top_spec = pl.BlockSpec((SUB, cols), lambda i: (last, 0))
-    full_spec = pl.BlockSpec((n, cols), lambda i: (0, 0))
-    near, far = pl.pallas_call(
+    edges = [pltpu.VMEM((SUB, cols), v.dtype) for v in fields]
+    near, far = call(
         edge_kernel,
-        grid=(1,),
-        out_shape=(f32((n, cols)), f32((n, cols))),
-        in_specs=[SMEM] + [low_spec] * 4 + [top_spec] * 4,
-        out_specs=(full_spec, full_spec),
-    )(where, *fields, *fields)
+        (f32((n, cols)),) * 2,
+        [HBM] * 4,
+        (VMEM,) * 2,
+        edges * 2 + [pltpu.SemaphoreType.DMA((8,))],
+    )(*fields)
 
     def own_chip(b, j):
         return (b, j ^ 1)
@@ -301,24 +319,25 @@
     x, f, c, columns = call(
         block_kernel,
         (f32((rows, cols)),) * 3 + (f32((2 * n, span)),),
-        [VMEM] * 4,
+        [HBM] * 4,
         (VMEM,) * 4,
+        [pltpu.VMEM((rows, cols), v.dtype) for v in fields] + [pltpu.SemaphoreType.DMA((4,))],
     )(*fields)
     halo, a, b = call(
         functools.partial(halo_kernel, rows),
         (f32((2 * n, cols)), f32((n, span)), f32((n, span))),
-        [SMEM] + [VMEM] * 3,
+        [VMEM] * 3,
         (VMEM,) * 3,
-    )(where, near, far, columns)
+    )(near, far, columns)
     a = swap(a, shape, even_pair)
     b = swap(b, shape, odd_pair)
     x, r, pairs = call(
         sweep_kernel,
         (f32((rows, cols)), f32((rows, cols)), f32((devices, LANE))),
-        [SMEM] + [VMEM] * 6,
+        [VMEM] * 6,
         (VMEM,) * 3,
         [pltpu.VMEM((tall, cols + LANE), jnp.float32)] * 3,
-    )(where, x, f, c, halo, a, b)
+    )(x, f, c, halo, a, b)
     pairs = lax.all_to_all(pairs, ("bx", "by"), 0, 0, tiled=True)
     cells = rows * cols * devices
     norm = call(functools.partial(norm_kernel, cells), f32((1,)), [VMEM], SMEM)(pairs)

time: 36.4 us -> 32.9 us (0.904)
  Pallas kernels: 10.2 us -> 4.64 us
  local copies, waits for them, and re-layouts: 1.19 us -> 3.64 us
  other arithmetic: 0.65 us -> 0 us
  blocking collectives: 14.7 us -> 15.2 us
    unnamed x8, local copies, waits for them, and re-layouts: 1.19 us -> 3.64 us
    pallas_call x2, Pallas kernels: 3.47 us -> 1.26 us  [the longest x1 1.1 us: per_device(): call(block_kernel, (f32((rows, cols)),) * 3 + (f32((2 * n, span)),), [HBM...]
    pallas_call x1, Pallas kernels: 1.62 us -> 0.15 us  [per_device(): call(functools.partial(halo_kernel, rows), (f32((2 * n, cols)), f32((n, s...]
    pallas_call x1, Pallas kernels: 3.75 us -> 2.56 us  [per_device(): call(sweep_kernel, (f32((rows, cols)), f32((rows, cols)), f32((devices, L...]
    pallas_call x1, Pallas kernels: 1.39 us -> 0.67 us  [per_device(): call(functools.partial(norm_kernel, cells), f32((1,)), [VMEM], SMEM)(pairs)]
    another operation x1 -> x0, other arithmetic: 0.65 us -> none  [per_device(): where = jnp.stack([by % 2, (by == high - 1).astype(jnp.int32), bx % 2])]
    all_to_all x1, blocking collectives: 14.7 us -> 15.2 us  [per_device(): pairs = lax.all_to_all(pairs, ('bx', 'by'), 0, 0, tiled=True)]
  transfers between devices with their start and end apart: 4 -> 4, of which waited for: 2 -> 2; matrix products, arithmetic and copies ran while one was open for 0% -> 0% of each run, Pallas kernels for 6% -> 3%
where the time goes in v2:
time: 32.9 us; the launch traced here: 32.7 us
  blocking collectives  15.2 us (46%)
  starting transfers between devices  5.25 us (16%)
  Pallas kernels  4.64 us (14%)
  local copies, waits for them, and re-layouts  3.64 us (11%)
  waiting for transfers between devices  3.24 us (10%)
  between operations  0.69 us (2%)
    all_to_all x1, blocking collectives, per_device(): pairs = lax.all_to_all(pairs, ('bx', 'by'), 0, 0, tiled=True)  15.2 us
    ppermute x4, starting transfers between devices, swap(): return lax.ppermute(value, ('bx', 'by'), moves)  5.25 us
    unnamed x8, local copies, waits for them, and re-layouts  3.64 us
    ppermute x4, waiting for transfers between devices, swap(): return lax.ppermute(value, ('bx', 'by'), moves)  3.24 us
    pallas_call x1, Pallas kernels, per_device(): call(sweep_kernel, (f32((rows, cols)), f32((rows, cols)), f32((devices, L...  2.56 us
    pallas_call x1, Pallas kernels, per_device(): call(block_kernel, (f32((rows, cols)),) * 3 + (f32((2 * n, span)),), [HBM...  1.1 us
    pallas_call x1, Pallas kernels, per_device(): call(functools.partial(norm_kernel, cells), f32((1,)), [VMEM], SMEM)(pairs)  0.67 us
  transfers between devices with their start and end apart: 4, of which 2 were waited for; matrix products, arithmetic and copies ran while one was open for 0% of the time, Pallas kernels for 3%

profile of v2, /device:TPU:0, one launch (start us, length us, event | category | flops | bytes accessed | tf_op | source)
XLA Modules:
  0.0 32.7 jit_solution(6911775289858947384)
XLA Ops:
  0.6 0.0 copy-start
  0.6 0.9 %copy-done = f32[152,256]{1,0:T(8,128)S(1)} copy-done((f32[152,256]{1,0:T(8,128)S(1)}, f32[152,256]{1,0:T(8,128)}, u32[]{:S(2)}) %copy-start) | copy-done | bytes 155672
  1.5 0.0 copy-start.1
  1.5 0.9 %copy-done.1 = f32[152,256]{1,0:T(8,128)S(1)} copy-done((f32[152,256]{1,0:T(8,128)S(1)}, f32[152,256]{1,0:T(8,128)}, u32[]{:S(2)}) %copy-start.1) | copy-done | bytes 155672
  2.5 0.0 copy-start.2
  2.5 0.9 %copy-done.2 = f32[152,256]{1,0:T(8,128)S(1)} copy-done((f32[152,256]{1,0:T(8,128)S(1)}, f32[152,256]{1,0:T(8,128)}, u32[]{:S(2)}) %copy-start.2) | copy-done | bytes 155672
  3.4 0.0 copy-start.3
  3.4 0.9 %copy-done.3 = s32[152,256]{1,0:T(8,128)S(1)} copy-done((s32[152,256]{1,0:T(8,128)S(1)}, s32[152,256]{1,0:T(8,128)}, u32[]{:S(2)}) %copy-start.3) | copy-done | bytes 155672
  4.3 0.2 shard_map.68
  4.4 0.6 %collective-permute-start = (f32[24,256]{1,0:T(8,128)S(1)}, f32[24,256]{1,0:T(8,128)S(1)}, u32[]{:S(2)}, u32[]{:S(2)}) collective-permute-start(f32[24,256]{1,0:T(8,128)S(1)} %get-tuple-element.18), channel_id=1, source_target_pairs={{0,1},{1,0},{2,3},{3,2},{4,5},{5,4},{6,7},{7,6},{8,9},{9,8},{10,11... | collective-permute-start | bytes 73736 | tf_op jit(solution)/shard_map/ppermute | solution.py:277
  5.0 0.7 %collective-permute-start.1 = (f32[24,256]{1,0:T(8,128)S(1)}, f32[24,256]{1,0:T(8,128)S(1)}, u32[]{:S(2)}, u32[]{:S(2)}) collective-permute-start(f32[24,256]{1,0:T(8,128)S(1)} %get-tuple-element.19), channel_id=1, source_target_pairs={{1,2},{2,1},{3,4},{4,3},{5,6},{6,5},{7,31},{9,10},{10,9},{11,12},{... | collective-permute-start | bytes 73736 | tf_op jit(solution)/shard_map/ppermute | solution.py:277
  5.7 1.1 %shard_map.67 = (f32[152,256]{1,0:T(8,128)S(1)}, f32[152,256]{1,0:T(8,128)S(1)}, f32[152,256]{1,0:T(8,128)S(1)}, f32[48,256]{1,0:T(8,128)S(1)}) custom-call(f32[152,256]{1,0:T(8,128)S(1)} %copy-done, f32[152,256]{1,0:T(8,128)S(1)} %copy-done.1, f32[152,256]{1,0:T(8,128)S(1)} %copy-done.2, s32[152,256]{1,0:T(8,128)S(1)} %copy-done.3), custom_call_target="tpu_custom_call" | custom-call | flops 100000 | tf_op jit(solution)/shard_map/pallas_call | solution.py:319
  6.8 0.0 collective-permute-done.near_ref
  6.8 0.0 collective-permute-done.1.far_ref
  6.8 0.2 shard_map.69
  7.0 2.5 %collective-permute-start.2 = (f32[24,256]{1,0:T(8,128)S(1)}, f32[24,256]{1,0:T(8,128)S(1)}, u32[]{:S(2)}, u32[]{:S(2)}) collective-permute-start(f32[24,256]{1,0:T(8,128)S(1)} %get-tuple-element.22), channel_id=1, source_target_pairs={{0,8},{1,9},{2,10},{3,11},{4,12},{5,13},{6,14},{7,15},{8,0},{9,1},... | collective-permute-start | bytes 73736 | tf_op jit(solution)/shard_map/ppermute | solution.py:277
  9.5 1.5 %collective-permute-start.3 = (f32[24,256]{1,0:T(8,128)S(1)}, f32[24,256]{1,0:T(8,128)S(1)}, u32[]{:S(2)}, u32[]{:S(2)}) collective-permute-start(f32[24,256]{1,0:T(8,128)S(1)} %get-tuple-element.23), channel_id=1, source_target_pairs={{0,24},{1,25},{2,26},{3,27},{4,28},{5,29},{6,30},{7,31},{8,16},{9,... | collective-permute-start | bytes 73736 | tf_op jit(solution)/shard_map/ppermute | solution.py:277
  11.0 0.3 collective-permute-done.2.a_ref
  11.3 2.9 %collective-permute-done.3.b_ref = f32[24,256]{1,0:T(8,128)S(1)} collective-permute-done((f32[24,256]{1,0:T(8,128)S(1)}, f32[24,256]{1,0:T(8,128)S(1)}, u32[]{:S(2)}, u32[]{:S(2)}) %collective-permute-start.3) | collective-permute-done | bytes 24608 | tf_op jit(solution)/shard_map/ppermute | solution.py:277
  14.2 2.6 %shard_map.70 = (f32[152,256]{1,0:T(8,128)}, f32[152,256]{1,0:T(8,128)}, f32[32,128]{1,0:T(8,128)S(1)}) custom-call(f32[152,256]{1,0:T(8,128)S(1)} %get-tuple-element.15.x_ref, f32[152,256]{1,0:T(8,128)S(1)} %get-tuple-element.16.f_ref, f32[152,256]{1,0:T(8,128)S(1)} %get-tuple-element.17.c_ref, f32[48,256]{1,0:T(8,128)S(1)} %get-tuple-element.21.halo_ref, ...), custom_call_target="tpu_custom_call" | custom-call | flops 100000 | tf_op jit(solution)/shard_map/pallas_call | solution.py:334
  16.8 15.2 %all_to_all.11 = f32[32,1,128]{2,1,0:T(1,128)S(1)} all-to-all(f32[32,1,128]{2,1,0:T(1,128)S(1)} %bitcast.6), channel_id=1, replica_groups=mesh['bx'=4,'by'=8] {'bx','by'}, dimensions={0} | all-to-all | bytes 32768 | tf_op jit(solution)/shard_map/all_to_all | solution.py:341
  32.0 0.7 %shard_map.71 = f32[1]{0:T(128)} custom-call(f32[32,128]{1,0:T(8,128)S(1)} %bitcast.5), custom_call_target="tpu_custom_call" | custom-call | flops 100000 | tf_op jit(solution)/shard_map/pallas_call | solution.py:343
Async XLA Ops:
  0.6 0.9 %copy-start = (f32[152,256]{1,0:T(8,128)S(1)}, f32[152,256]{1,0:T(8,128)}, u32[]{:S(2)}) copy-start(f32[152,256]{1,0:T(8,128)} %refs_0_.3) | copy-start | bytes 466948
  1.5 0.9 %copy-start.1 = (f32[152,256]{1,0:T(8,128)S(1)}, f32[152,256]{1,0:T(8,128)}, u32[]{:S(2)}) copy-start(f32[152,256]{1,0:T(8,128)} %refs_1_.3) | copy-start | bytes 466948
  2.5 0.9 %copy-start.2 = (f32[152,256]{1,0:T(8,128)S(1)}, f32[152,256]{1,0:T(8,128)}, u32[]{:S(2)}) copy-start(f32[152,256]{1,0:T(8,128)} %refs_2_.3) | copy-start | bytes 466948
  3.4 0.9 %copy-start.3 = (s32[152,256]{1,0:T(8,128)S(1)}, s32[152,256]{1,0:T(8,128)}, u32[]{:S(2)}) copy-start(s32[152,256]{1,0:T(8,128)} %refs_3_.3) | copy-start | bytes 466948
  4.4 2.3 %collective-permute-start = (f32[24,256]{1,0:T(8,128)S(1)}, f32[24,256]{1,0:T(8,128)S(1)}, u32[]{:S(2)}, u32[]{:S(2)}) collective-permute-start(f32[24,256]{1,0:T(8,128)S(1)} %get-tuple-element.18), channel_id=1, source_target_pairs={{0,1},{1,0},{2,3},{3,2},{4,5},{5,4},{6,7},{7,6},{8,9},{9,8},{10,11... | collective-permute-start | bytes 73736 | tf_op jit(solution)/shard_map/ppermute | solution.py:277
  5.0 1.8 %collective-permute-start.1 = (f32[24,256]{1,0:T(8,128)S(1)}, f32[24,256]{1,0:T(8,128)S(1)}, u32[]{:S(2)}, u32[]{:S(2)}) collective-permute-start(f32[24,256]{1,0:T(8,128)S(1)} %get-tuple-element.19), channel_id=1, source_target_pairs={{1,2},{2,1},{3,4},{4,3},{5,6},{6,5},{7,31},{9,10},{10,9},{11,12},{... | collective-permute-start | bytes 73736 | tf_op jit(solution)/shard_map/ppermute | solution.py:277
  7.0 4.4 %collective-permute-start.2 = (f32[24,256]{1,0:T(8,128)S(1)}, f32[24,256]{1,0:T(8,128)S(1)}, u32[]{:S(2)}, u32[]{:S(2)}) collective-permute-start(f32[24,256]{1,0:T(8,128)S(1)} %get-tuple-element.22), channel_id=1, source_target_pairs={{0,8},{1,9},{2,10},{3,11},{4,12},{5,13},{6,14},{7,15},{8,0},{9,1},... | collective-permute-start | bytes 73736 | tf_op jit(solution)/shard_map/ppermute | solution.py:277
  9.5 4.7 %collective-permute-start.3 = (f32[24,256]{1,0:T(8,128)S(1)}, f32[24,256]{1,0:T(8,128)S(1)}, u32[]{:S(2)}, u32[]{:S(2)}) collective-permute-start(f32[24,256]{1,0:T(8,128)S(1)} %get-tuple-element.23), channel_id=1, source_target_pairs={{0,24},{1,25},{2,26},{3,27},{4,28},{5,29},{6,30},{7,31},{8,16},{9,... | collective-permute-start | bytes 73736 | tf_op jit(solution)/shard_map/ppermute | solution.py:277

commit v3 on v2

--- a/solution.py
+++ b/solution.py
@@ -287,7 +287,8 @@
     tall = rows + 2 * SUB
     span = -(-tall // LANE) * LANE
     f32 = functools.partial(jax.ShapeDtypeStruct, dtype=jnp.float32)
-    fields = (forcing, guess, shift, ocean)
+    held = functools.partial(pltpu.VMEM, dtype=jnp.float32)
+    fields = [pltpu.with_memory_space_constraint(v, pltpu.HBM) for v in (forcing, guess, shift, ocean)]
     edges = [pltpu.VMEM((SUB, cols), v.dtype) for v in fields]
     near, far = call(
         edge_kernel,
@@ -333,7 +334,7 @@
     b = swap(b, shape, odd_pair)
     x, r, pairs = call(
         sweep_kernel,
-        (f32((rows, cols)), f32((rows, cols)), f32((devices, LANE))),
+        (held((rows, cols)), held((rows, cols)), held((devices, LANE))),
         [VMEM] * 6,
         (VMEM,) * 3,
         [pltpu.VMEM((tall, cols + LANE), jnp.float32)] * 3,

time: 32.9 us -> 30.4 us (0.924)
  blocking collectives: 15.2 us -> 0 us
  starting transfers between devices: 5.25 us -> 13.2 us
  waiting for transfers between devices: 3.24 us -> 9.07 us
  local copies, waits for them, and re-layouts: 3.64 us -> 1.33 us
  Pallas kernels: 4.64 us -> 5.82 us
    all_to_all x1 -> x0, blocking collectives: 15.2 us -> none  [per_device(): pairs = lax.all_to_all(pairs, ('bx', 'by'), 0, 0, tiled=True)]
    all_to_all x0 -> x1, starting transfers between devices: none -> 7.92 us  [per_device(): pairs = lax.all_to_all(pairs, ('bx', 'by'), 0, 0, tiled=True)]
    all_to_all x0 -> x1, waiting for transfers between devices: none -> 5.83 us  [per_device(): pairs = lax.all_to_all(pairs, ('bx', 'by'), 0, 0, tiled=True)]
    unnamed x8 -> x2, local copies, waits for them, and re-layouts: 3.64 us -> 1.33 us
    pallas_call x1, Pallas kernels: 0.16 us -> 0.89 us  [per_device(): call(edge_kernel, (f32((n, cols)),) * 2, [HBM] * 4, (VMEM,) * 2, edges *...]
    pallas_call x1, Pallas kernels: 1.1 us -> 1.43 us  [per_device(): call(block_kernel, (f32((rows, cols)),) * 3 + (f32((2 * n, span)),), [HBM...]
  transfers between devices with their start and end apart: 4 -> 5, of which waited for: 2 -> 3; matrix products, arithmetic and copies ran while one was open for 0% -> 4% of each run, Pallas kernels for 3% -> 5%
where the time goes in v3:
time: 30.4 us; the launch traced here: 30.1 us
  starting transfers between devices  13.2 us (43%)
  waiting for transfers between devices  9.07 us (30%)
  Pallas kernels  5.82 us (19%)
  local copies, waits for them, and re-layouts  1.33 us (4%)
  between operations  0.68 us (2%)
    all_to_all x1, starting transfers between devices, per_device(): pairs = lax.all_to_all(pairs, ('bx', 'by'), 0, 0, tiled=True)  7.92 us
    all_to_all x1, waiting for transfers between devices, per_device(): pairs = lax.all_to_all(pairs, ('bx', 'by'), 0, 0, tiled=True)  5.83 us
    ppermute x4, starting transfers between devices, swap(): return lax.ppermute(value, ('bx', 'by'), moves)  5.25 us
    ppermute x4, waiting for transfers between devices, swap(): return lax.ppermute(value, ('bx', 'by'), moves)  3.24 us
    pallas_call x1, Pallas kernels, per_device(): call(sweep_kernel, (held((rows, cols)), held((rows, cols)), held((devices...  2.67 us
    pallas_call x1, Pallas kernels, per_device(): call(block_kernel, (f32((rows, cols)),) * 3 + (f32((2 * n, span)),), [HBM...  1.43 us
    unnamed x2, local copies, waits for them, and re-layouts  1.33 us
    pallas_call x1, Pallas kernels, per_device(): call(edge_kernel, (f32((n, cols)),) * 2, [HBM] * 4, (VMEM,) * 2, edges *...  0.89 us
  transfers between devices with their start and end apart: 5, of which 3 were waited for; matrix products, arithmetic and copies ran while one was open for 4% of the time, Pallas kernels for 5%

profile of v3, /device:TPU:0, one launch (start us, length us, event | category | flops | bytes accessed | tf_op | source)
XLA Modules:
  0.0 30.1 jit_solution(4206860192827741109)
XLA Ops:
  0.6 0.9 %shard_map.68 = (f32[24,256]{1,0:T(8,128)S(1)}, f32[24,256]{1,0:T(8,128)S(1)}) custom-call(f32[152,256]{1,0:T(8,128)} %refs_0_.3, f32[152,256]{1,0:T(8,128)} %refs_1_.3, f32[152,256]{1,0:T(8,128)} %refs_2_.3, s32[152,256]{1,0:T(8,128)} %refs_3_.3), custom_call_target="tpu_custom_call" | custom-call | flops 100000 | tf_op jit(solution)/shard_map/pallas_call | solution.py:293
  1.5 0.6 %collective-permute-start = (f32[24,256]{1,0:T(8,128)S(1)}, f32[24,256]{1,0:T(8,128)S(1)}, u32[]{:S(2)}, u32[]{:S(2)}) collective-permute-start(f32[24,256]{1,0:T(8,128)S(1)} %get-tuple-element.18), channel_id=1, source_target_pairs={{0,1},{1,0},{2,3},{3,2},{4,5},{5,4},{6,7},{7,6},{8,9},{9,8},{10,11... | collective-permute-start | bytes 73736 | tf_op jit(solution)/shard_map/ppermute | solution.py:277
  2.1 0.7 %collective-permute-start.1 = (f32[24,256]{1,0:T(8,128)S(1)}, f32[24,256]{1,0:T(8,128)S(1)}, u32[]{:S(2)}, u32[]{:S(2)}) collective-permute-start(f32[24,256]{1,0:T(8,128)S(1)} %get-tuple-element.19), channel_id=1, source_target_pairs={{1,2},{2,1},{3,4},{4,3},{5,6},{6,5},{7,31},{9,10},{10,9},{11,12},{... | collective-permute-start | bytes 73736 | tf_op jit(solution)/shard_map/ppermute | solution.py:277
  2.7 1.4 %shard_map.67 = (f32[152,256]{1,0:T(8,128)S(1)}, f32[152,256]{1,0:T(8,128)S(1)}, f32[152,256]{1,0:T(8,128)S(1)}, f32[48,256]{1,0:T(8,128)S(1)}) custom-call(f32[152,256]{1,0:T(8,128)} %refs_0_.3, f32[152,256]{1,0:T(8,128)} %refs_1_.3, f32[152,256]{1,0:T(8,128)} %refs_2_.3, s32[152,256]{1,0:T(8,128)} %refs_3_.3), custom_call_target="tpu_custom_call" | custom-call | flops 100000 | tf_op jit(solution)/shard_map/pallas_call | solution.py:320
  4.2 0.0 collective-permute-done.near_ref
  4.2 0.0 collective-permute-done.1.far_ref
  4.2 0.2 shard_map.69
  4.4 2.5 %collective-permute-start.2 = (f32[24,256]{1,0:T(8,128)S(1)}, f32[24,256]{1,0:T(8,128)S(1)}, u32[]{:S(2)}, u32[]{:S(2)}) collective-permute-start(f32[24,256]{1,0:T(8,128)S(1)} %get-tuple-element.22), channel_id=1, source_target_pairs={{0,8},{1,9},{2,10},{3,11},{4,12},{5,13},{6,14},{7,15},{8,0},{9,1},... | collective-permute-start | bytes 73736 | tf_op jit(solution)/shard_map/ppermute | solution.py:277
  6.9 1.5 %collective-permute-start.3 = (f32[24,256]{1,0:T(8,128)S(1)}, f32[24,256]{1,0:T(8,128)S(1)}, u32[]{:S(2)}, u32[]{:S(2)}) collective-permute-start(f32[24,256]{1,0:T(8,128)S(1)} %get-tuple-element.23), channel_id=1, source_target_pairs={{0,24},{1,25},{2,26},{3,27},{4,28},{5,29},{6,30},{7,31},{8,16},{9,... | collective-permute-start | bytes 73736 | tf_op jit(solution)/shard_map/ppermute | solution.py:277
  8.4 0.3 %collective-permute-done.2.a_ref = f32[24,256]{1,0:T(8,128)S(1)} collective-permute-done((f32[24,256]{1,0:T(8,128)S(1)}, f32[24,256]{1,0:T(8,128)S(1)}, u32[]{:S(2)}, u32[]{:S(2)}) %collective-permute-start.2) | collective-permute-done | bytes 24608 | tf_op jit(solution)/shard_map/ppermute | solution.py:277
  8.7 2.9 %collective-permute-done.3.b_ref = f32[24,256]{1,0:T(8,128)S(1)} collective-permute-done((f32[24,256]{1,0:T(8,128)S(1)}, f32[24,256]{1,0:T(8,128)S(1)}, u32[]{:S(2)}, u32[]{:S(2)}) %collective-permute-start.3) | collective-permute-done | bytes 24608 | tf_op jit(solution)/shard_map/ppermute | solution.py:277
  11.6 2.7 %shard_map.70 = (f32[152,256]{1,0:T(8,128)S(1)}, f32[152,256]{1,0:T(8,128)S(1)}, f32[32,128]{1,0:T(8,128)}) custom-call(f32[152,256]{1,0:T(8,128)S(1)} %get-tuple-element.15.x_ref, f32[152,256]{1,0:T(8,128)S(1)} %get-tuple-element.16.f_ref, f32[152,256]{1,0:T(8,128)S(1)} %get-tuple-element.17.c_ref, f32[48,256]{1,0:T(8,128)S(1)} %get-tuple-element.21.halo_ref, ...), custom_call_target="tpu_custom_call" | custom-call | flops 100000 | tf_op jit(solution)/shard_map/pallas_call | solution.py:335
  14.3 7.9 %all-to-all-start = ((f32[32,1,128]{2,1,0:T(1,128)}), f32[32,1,128]{2,1,0:T(1,128)S(1)}, u32[]{:S(2)}, u32[]{:S(2)}) async-start(f32[32,1,128]{2,1,0:T(1,128)} %bitcast.1), calls=%async_computation | async-start | bytes 32768 | tf_op jit(solution)/shard_map/all_to_all | solution.py:342
  22.2 0.7 %copy.8 = f32[152,256]{1,0:T(8,128)} copy(f32[152,256]{1,0:T(8,128)S(1)} %get-tuple-element.27) | data formatting | bytes 311296
  22.9 0.7 %copy.9 = f32[152,256]{1,0:T(8,128)} copy(f32[152,256]{1,0:T(8,128)S(1)} %get-tuple-element.28) | data formatting | bytes 311296
  23.6 5.8 %all-to-all-done = f32[32,1,128]{2,1,0:T(1,128)S(1)} async-done(((f32[32,1,128]{2,1,0:T(1,128)}), f32[32,1,128]{2,1,0:T(1,128)S(1)}, u32[]{:S(2)}, u32[]{:S(2)}) %all-to-all-start) | async-done | bytes 16416 | tf_op jit(solution)/shard_map/all_to_all | solution.py:342
  29.4 0.7 %shard_map.71 = f32[1]{0:T(128)} custom-call(f32[32,128]{1,0:T(8,128)S(1)} %bitcast.5), custom_call_target="tpu_custom_call" | custom-call | flops 100000 | tf_op jit(solution)/shard_map/pallas_call | solution.py:344
Async XLA Ops:
  1.5 2.7 %collective-permute-start = (f32[24,256]{1,0:T(8,128)S(1)}, f32[24,256]{1,0:T(8,128)S(1)}, u32[]{:S(2)}, u32[]{:S(2)}) collective-permute-start(f32[24,256]{1,0:T(8,128)S(1)} %get-tuple-element.18), channel_id=1, source_target_pairs={{0,1},{1,0},{2,3},{3,2},{4,5},{5,4},{6,7},{7,6},{8,9},{9,8},{10,11... | collective-permute-start | bytes 73736 | tf_op jit(solution)/shard_map/ppermute | solution.py:277
  2.1 2.1 %collective-permute-start.1 = (f32[24,256]{1,0:T(8,128)S(1)}, f32[24,256]{1,0:T(8,128)S(1)}, u32[]{:S(2)}, u32[]{:S(2)}) collective-permute-start(f32[24,256]{1,0:T(8,128)S(1)} %get-tuple-element.19), channel_id=1, source_target_pairs={{1,2},{2,1},{3,4},{4,3},{5,6},{6,5},{7,31},{9,10},{10,9},{11,12},{... | collective-permute-start | bytes 73736 | tf_op jit(solution)/shard_map/ppermute | solution.py:277
  4.4 4.4 %collective-permute-start.2 = (f32[24,256]{1,0:T(8,128)S(1)}, f32[24,256]{1,0:T(8,128)S(1)}, u32[]{:S(2)}, u32[]{:S(2)}) collective-permute-start(f32[24,256]{1,0:T(8,128)S(1)} %get-tuple-element.22), channel_id=1, source_target_pairs={{0,8},{1,9},{2,10},{3,11},{4,12},{5,13},{6,14},{7,15},{8,0},{9,1},... | collective-permute-start | bytes 73736 | tf_op jit(solution)/shard_map/ppermute | solution.py:277
  6.9 4.7 %collective-permute-start.3 = (f32[24,256]{1,0:T(8,128)S(1)}, f32[24,256]{1,0:T(8,128)S(1)}, u32[]{:S(2)}, u32[]{:S(2)}) collective-permute-start(f32[24,256]{1,0:T(8,128)S(1)} %get-tuple-element.23), channel_id=1, source_target_pairs={{0,24},{1,25},{2,26},{3,27},{4,28},{5,29},{6,30},{7,31},{8,16},{9,... | collective-permute-start | bytes 73736 | tf_op jit(solution)/shard_map/ppermute | solution.py:277
  14.3 15.1 %all-to-all-start = ((f32[32,1,128]{2,1,0:T(1,128)}), f32[32,1,128]{2,1,0:T(1,128)S(1)}, u32[]{:S(2)}, u32[]{:S(2)}) async-start(f32[32,1,128]{2,1,0:T(1,128)} %bitcast.1), calls=%async_computation | async-start | bytes 32768 | tf_op jit(solution)/shard_map/all_to_all | solution.py:342

commit v4 on v3

--- a/solution.py
+++ b/solution.py
@@ -185,28 +185,9 @@
     return total
 
 
-def sweep_kernel(x_ref, f_ref, c_ref, halo_ref, a_ref, b_ref, out_x_ref, out_r_ref, pair_ref, d_s, r_s, c_s):
-    odd_x = is_odd("bx")
-    rows, cols = x_ref.shape
-    n = FIELDS * SUB
-    tiles, inner = d_s.shape[0] // SUB, rows // SUB
-    wide = cols + LANE
-    high = d_s.shape[0]
-    a, b = a_ref[...], b_ref[...]
-    left, right = jnp.where(odd_x, a, b), jnp.where(odd_x, b, a)
-    pieces = []
-    for f in range(FIELDS):
-        at = slice(f * SUB, (f + 1) * SUB)
-        pieces += [left[at], right[at]]
-    pieces.append(jnp.zeros((LANE - 2 * n, a.shape[1]), jnp.float32))
-    sides = jnp.concatenate(pieces, axis=0).T
-    for f, (ref, main) in enumerate(((d_s, x_ref), (r_s, f_ref), (c_s, c_ref))):
-        at = slice(f * SUB, (f + 1) * SUB)
-        ref[0:rows, 0:cols] = main[...]
-        ref[rows : rows + SUB, 0:cols] = halo_ref[at, :]
-        ref[rows + SUB : high, 0:cols] = halo_ref[n + f * SUB : n + (f + 1) * SUB, :]
-        ref[:, cols:wide] = pltpu.roll(sides[0:high], LANE - (2 * f + 1) * SUB, 1)
-
+def sweeps(inner, x_s, d_s, r_s, c_s, weigh):
+    tall, wide = d_s.shape
+    tiles = tall // SUB
     theta, steps = coefficients()
     row_id = lax.broadcasted_iota(jnp.int32, (SUB, wide), 0)
     first_row, last_row = row_id == 0, row_id == SUB - 1
@@ -242,28 +223,78 @@
                     d = keep * v + gain * r
                 d_s[at, :] = d
                 if i < inner:
-                    old = x_ref[at, :] if sweep == 0 else out_x_ref[at, :]
-                    out_x_ref[at, :] = old + d[:, :cols]
+                    x_s[at, :] = (v if sweep == 0 else x_s[at, :]) + d
             elif i < inner:
-                r = r[:, :cols]
-                out_r_ref[at, :] = r
+                r_s[at, :] = r
+                r = jnp.where(weigh, r, jnp.zeros_like(r))
                 squares.append(jnp.sum(r * r, axis=1, keepdims=True))
             before, now = now, after
     zero = jnp.zeros_like(squares[0])
-    upper, lower = pair_total([(q, zero) for q in squares])
+    return pair_total([(q, zero) for q in squares])
+
+
+def interior_kernel(x_ref, f_ref, c_ref, halo_ref, out_x_ref, out_r_ref, pair_ref, strip_x, strip_r, strip_c, d_s, c_s):
+    rows, cols = x_ref.shape
+    high = d_s.shape[0]
+    n = FIELDS * SUB
+    lane = lax.broadcasted_iota(jnp.int32, (high, LANE), 1)
+    left, right = (lane >= LANE // 2) & (lane < LANE // 2 + 2 * SUB), lane >= LANE - 2 * SUB
+    for f, (ref, main, strip) in enumerate(((d_s, x_ref, strip_x), (out_r_ref, f_ref, strip_r), (c_s, c_ref, strip_c))):
+        ref[0:rows, :] = main[...]
+        ref[rows : rows + SUB, :] = halo_ref[f * SUB : (f + 1) * SUB, :]
+        ref[rows + SUB : high, :] = halo_ref[n + f * SUB : n + (f + 1) * SUB, :]
+        ends = jnp.where(left, pltpu.roll(ref[:, 0:LANE], LANE // 2, 1), 0.0)
+        strip[...] = jnp.where(right, ref[:, cols - LANE : cols], ends)
+    column = lax.broadcasted_iota(jnp.int32, (SUB, cols), 1)
+    weigh = (column >= SUB) & (column < cols - SUB)
+    upper, lower = sweeps(rows // SUB, out_x_ref, d_s, out_r_ref, c_s, weigh)
+    pair_ref[0:SUB, :] = jnp.broadcast_to(upper, (SUB, LANE))
+    pair_ref[SUB : 2 * SUB, :] = jnp.broadcast_to(lower, (SUB, LANE))
+
+
+def strip_kernel(strip_x, strip_r, strip_c, a_ref, b_ref, pair_ref, out_x_ref, out_r_ref, pairs_ref, d_s, c_s):
+    odd_x = is_odd("bx")
+    high = d_s.shape[0]
+    n = FIELDS * SUB
+    middle = LANE // 2
+    a, b = a_ref[...], b_ref[...]
+    left, right = jnp.where(odd_x, a, b), jnp.where(odd_x, b, a)
+    gap = jnp.zeros((middle - SUB - n, a.shape[1]), jnp.float32)
+    rest = jnp.zeros((middle + SUB - n, a.shape[1]), jnp.float32)
+    sides = jnp.concatenate([right, gap, left, rest], axis=0).T[0:high]
+    lane = lax.broadcasted_iota(jnp.int32, (high, LANE), 1)
+    ghost = (lane < SUB) | ((lane >= middle - SUB) & (lane < middle))
+    for f, (ref, strip) in enumerate(((d_s, strip_x), (out_r_ref, strip_r), (c_s, strip_c))):
+        side = pltpu.roll(sides, LANE - f * SUB, 1) if f else sides
+        ref[...] = jnp.where(ghost, side, strip[...])
     lane = lax.broadcasted_iota(jnp.int32, (SUB, LANE), 1)
-    tile = jnp.where(lane < LANE // 2, upper, lower)
-    for i in range(pair_ref.shape[0] // SUB):
-        pair_ref[i * SUB : (i + 1) * SUB, :] = tile
-
-
-def norm_kernel(cells, pairs_ref, out_ref):
+    weigh = ((lane >= middle) & (lane < middle + SUB)) | (lane >= LANE - SUB)
+    ends = sweeps(out_x_ref.shape[0] // SUB, out_x_ref, d_s, out_r_ref, c_s, weigh)
+    upper, lower = pair_add(ends, (pair_ref[0:SUB, :], pair_ref[SUB : 2 * SUB, :]))
+    tile = jnp.where(lane < middle, upper, lower)
+    for i in range(pairs_ref.shape[0] // SUB):
+        pairs_ref[i * SUB : (i + 1) * SUB, :] = tile
+
+
+def norm_kernel(cells, pairs_ref, x_ref, r_ref, strip_x, strip_r, x_hbm, r_hbm, norm_ref, x_s, r_s, sem):
+    rows, cols = x_s.shape
+    lane = lax.broadcasted_iota(jnp.int32, (rows, LANE), 1)
+    copies = []
+    for i, (main, strip, joined, out) in enumerate(((x_ref, strip_x, x_s, x_hbm), (r_ref, strip_r, r_s, r_hbm))):
+        joined[...] = main[0:rows, :]
+        ends = strip[0:rows, :]
+        joined[:, 0:LANE] = jnp.where(lane < SUB, pltpu.roll(ends, LANE // 2, 1), joined[:, 0:LANE])
+        joined[:, cols - LANE : cols] = jnp.where(lane >= LANE - SUB, ends, joined[:, cols - LANE : cols])
+        copies.append(pltpu.make_async_copy(joined, out, sem.at[i]))
+        copies[i].start()
     pairs = []
     for i in range(pairs_ref.shape[0] // SUB):
         upper = pairs_ref[i * SUB : (i + 1) * SUB, :]
         pairs.append((upper, pltpu.roll(upper, LANE // 2, 1)))
     upper, lower = pair_total(pairs)
-    out_ref[0] = jnp.sqrt((upper + lower) * (1.0 / cells))[0, 0]
+    norm_ref[0] = jnp.sqrt((upper + lower) * (1.0 / cells))[0, 0]
+    for copy in copies:
+        copy.wait()
 
 
 def swap(value, mesh_shape, partner):
@@ -332,16 +363,29 @@
     )(near, far, columns)
     a = swap(a, shape, even_pair)
     b = swap(b, shape, odd_pair)
-    x, r, pairs = call(
-        sweep_kernel,
-        (held((rows, cols)), held((rows, cols)), held((devices, LANE))),
+    high = (tall, LANE)
+    x, r, pair, *strips = call(
+        interior_kernel,
+        (held((rows, cols)), held((tall, cols)), held((2 * SUB, LANE))) + (held(high),) * 3,
+        [VMEM] * 4,
+        (VMEM,) * 6,
+        [pltpu.VMEM((tall, cols), jnp.float32)] * 2,
+    )(x, f, c, halo)
+    strip_x, strip_r, pairs = call(
+        strip_kernel,
+        (held((rows, LANE)), held(high), held((devices, LANE))),
         [VMEM] * 6,
         (VMEM,) * 3,
-        [pltpu.VMEM((tall, cols + LANE), jnp.float32)] * 3,
-    )(x, f, c, halo, a, b)
+        [pltpu.VMEM(high, jnp.float32)] * 2,
+    )(*strips, a, b, pair)
     pairs = lax.all_to_all(pairs, ("bx", "by"), 0, 0, tiled=True)
-    cells = rows * cols * devices
-    norm = call(functools.partial(norm_kernel, cells), f32((1,)), [VMEM], SMEM)(pairs)
+    x, r, norm = call(
+        functools.partial(norm_kernel, rows * cols * devices),
+        (f32((rows, cols)), f32((rows, cols)), f32((1,))),
+        [VMEM] * 5,
+        (HBM, HBM, SMEM),
+        [pltpu.VMEM((rows, cols), jnp.float32)] * 2 + [pltpu.SemaphoreType.DMA((2,))],
+    )(pairs, x, r, strip_x, strip_r)
     return (x, r, norm[0])
 
 

time: 30.4 us -> 29.1 us (0.957)
  blocking collectives: 0 us -> 14.9 us
  starting transfers between devices: 13.2 us -> 5.25 us
  waiting for transfers between devices: 9.07 us -> 1.57 us
  local copies, waits for them, and re-layouts: 1.33 us -> 0 us
  Pallas kernels: 5.82 us -> 6.48 us
    all_to_all x0 -> x1, blocking collectives: none -> 14.9 us  [per_device(): pairs = lax.all_to_all(pairs, ('bx', 'by'), 0, 0, tiled=True)]
    all_to_all x1 -> x0, starting transfers between devices: 7.92 us -> none  [per_device(): pairs = lax.all_to_all(pairs, ('bx', 'by'), 0, 0, tiled=True)]
    all_to_all x1 -> x0, waiting for transfers between devices: 5.83 us -> none  [per_device(): pairs = lax.all_to_all(pairs, ('bx', 'by'), 0, 0, tiled=True)]
    ppermute x4, waiting for transfers between devices: 3.24 us -> 1.57 us  [swap(): return lax.ppermute(value, ('bx', 'by'), moves)]
    unnamed x2 -> x0, local copies, waits for them, and re-layouts: 1.33 us -> none
    pallas_call x2 -> x3, Pallas kernels: 3.34 us -> 3.99 us  [the longest x1 1.67 us: per_device(): call(interior_kernel, (held((rows, cols)), held((tall, cols)), held((2 *...]
  transfers between devices with their start and end apart: 5 -> 4, of which waited for: 3 -> 1; matrix products, arithmetic and copies ran while one was open for 4% -> 0% of each run, Pallas kernels for 5% -> 11%
where the time goes in v4:
time: 29.1 us; the launch traced here: 28.9 us
  blocking collectives  14.9 us (51%)
  Pallas kernels  6.48 us (22%)
  starting transfers between devices  5.25 us (18%)
  waiting for transfers between devices  1.57 us (5%)
  between operations  0.67 us (2%)
    all_to_all x1, blocking collectives, per_device(): pairs = lax.all_to_all(pairs, ('bx', 'by'), 0, 0, tiled=True)  14.9 us
    ppermute x4, starting transfers between devices, swap(): return lax.ppermute(value, ('bx', 'by'), moves)  5.25 us
    pallas_call x1, Pallas kernels, per_device(): call(interior_kernel, (held((rows, cols)), held((tall, cols)), held((2 *...  1.67 us
    ppermute x4, waiting for transfers between devices, swap(): return lax.ppermute(value, ('bx', 'by'), moves)  1.57 us
    pallas_call x1, Pallas kernels, per_device(): call(block_kernel, (f32((rows, cols)),) * 3 + (f32((2 * n, span)),), [HBM...  1.43 us
    pallas_call x1, Pallas kernels, per_device(): call(functools.partial(norm_kernel, rows * cols * devices), (f32((rows, c...  1.35 us
    pallas_call x1, Pallas kernels, per_device(): call(strip_kernel, (held((rows, LANE)), held(high), held((devices, LANE))...  0.98 us
    pallas_call x1, Pallas kernels, per_device(): call(edge_kernel, (f32((n, cols)),) * 2, [HBM] * 4, (VMEM,) * 2, edges *...  0.89 us
  transfers between devices with their start and end apart: 4, of which 1 were waited for; matrix products, arithmetic and copies ran while one was open for 0% of the time, Pallas kernels for 11%

profile of v4, /device:TPU:0, one launch (start us, length us, event | category | flops | bytes accessed | tf_op | source)
XLA Modules:
  0.0 28.9 jit_solution(17798646793672507568)
XLA Ops:
  0.6 0.9 %shard_map.68 = (f32[24,256]{1,0:T(8,128)S(1)}, f32[24,256]{1,0:T(8,128)S(1)}) custom-call(f32[152,256]{1,0:T(8,128)} %refs_0_.3, f32[152,256]{1,0:T(8,128)} %refs_1_.3, f32[152,256]{1,0:T(8,128)} %refs_2_.3, s32[152,256]{1,0:T(8,128)} %refs_3_.3), custom_call_target="tpu_custom_call" | custom-call | flops 100000 | tf_op jit(solution)/shard_map/pallas_call | solution.py:324
  1.5 0.6 %collective-permute-start = (f32[24,256]{1,0:T(8,128)S(1)}, f32[24,256]{1,0:T(8,128)S(1)}, u32[]{:S(2)}, u32[]{:S(2)}) collective-permute-start(f32[24,256]{1,0:T(8,128)S(1)} %get-tuple-element.27), channel_id=1, source_target_pairs={{0,1},{1,0},{2,3},{3,2},{4,5},{5,4},{6,7},{7,6},{8,9},{9,8},{10,11... | collective-permute-start | bytes 73736 | tf_op jit(solution)/shard_map/ppermute | solution.py:308
  2.1 0.7 %collective-permute-start.1 = (f32[24,256]{1,0:T(8,128)S(1)}, f32[24,256]{1,0:T(8,128)S(1)}, u32[]{:S(2)}, u32[]{:S(2)}) collective-permute-start(f32[24,256]{1,0:T(8,128)S(1)} %get-tuple-element.28), channel_id=1, source_target_pairs={{1,2},{2,1},{3,4},{4,3},{5,6},{6,5},{7,31},{9,10},{10,9},{11,12},{... | collective-permute-start | bytes 73736 | tf_op jit(solution)/shard_map/ppermute | solution.py:308
  2.7 1.4 %shard_map.67 = (f32[152,256]{1,0:T(8,128)S(1)}, f32[152,256]{1,0:T(8,128)S(1)}, f32[152,256]{1,0:T(8,128)S(1)}, f32[48,256]{1,0:T(8,128)S(1)}) custom-call(f32[152,256]{1,0:T(8,128)} %refs_0_.3, f32[152,256]{1,0:T(8,128)} %refs_1_.3, f32[152,256]{1,0:T(8,128)} %refs_2_.3, s32[152,256]{1,0:T(8,128)} %refs_3_.3), custom_call_target="tpu_custom_call" | custom-call | flops 100000 | tf_op jit(solution)/shard_map/pallas_call | solution.py:351
  4.2 0.0 collective-permute-done.near_ref
  4.2 0.0 collective-permute-done.1.far_ref
  4.2 0.2 shard_map.69
  4.4 2.5 %collective-permute-start.2 = (f32[24,256]{1,0:T(8,128)S(1)}, f32[24,256]{1,0:T(8,128)S(1)}, u32[]{:S(2)}, u32[]{:S(2)}) collective-permute-start(f32[24,256]{1,0:T(8,128)S(1)} %get-tuple-element.34), channel_id=1, source_target_pairs={{0,8},{1,9},{2,10},{3,11},{4,12},{5,13},{6,14},{7,15},{8,0},{9,1},... | collective-permute-start | bytes 73736 | tf_op jit(solution)/shard_map/ppermute | solution.py:308
  6.9 1.5 %collective-permute-start.3 = (f32[24,256]{1,0:T(8,128)S(1)}, f32[24,256]{1,0:T(8,128)S(1)}, u32[]{:S(2)}, u32[]{:S(2)}) collective-permute-start(f32[24,256]{1,0:T(8,128)S(1)} %get-tuple-element.35), channel_id=1, source_target_pairs={{0,24},{1,25},{2,26},{3,27},{4,28},{5,29},{6,30},{7,31},{8,16},{9,... | collective-permute-start | bytes 73736 | tf_op jit(solution)/shard_map/ppermute | solution.py:308
  8.4 1.7 %shard_map.70 = (f32[152,256]{1,0:T(8,128)S(1)}, f32[168,256]{1,0:T(8,128)S(1)}, f32[16,128]{1,0:T(8,128)S(1)}, f32[168,128]{1,0:T(8,128)S(1)}, f32[168,128]{1,0:T(8,128)S(1)}, /*index=5*/f32[168,128]{1,0:T(8,128)S(1)}) custom-call(f32[152,256]{1,0:T(8,128)S(1)} %get-tuple-element.24.x_ref, f32[152,256]{1,0:T(8,128)S(1)} %get-tuple-element.25.f_ref, ...), custom_call_target="tpu_custom_call" | custom-call | flops 100000 | tf_op jit(solution)/shard_map/pallas_call | solution.py:367
  10.1 0.0 collective-permute-done.2.a_ref
  10.1 1.6 %collective-permute-done.3.b_ref = f32[24,256]{1,0:T(8,128)S(1)} collective-permute-done((f32[24,256]{1,0:T(8,128)S(1)}, f32[24,256]{1,0:T(8,128)S(1)}, u32[]{:S(2)}, u32[]{:S(2)}) %collective-permute-start.3) | collective-permute-done | bytes 24608 | tf_op jit(solution)/shard_map/ppermute | solution.py:308
  11.6 1.0 %shard_map.71 = (f32[152,128]{1,0:T(8,128)S(1)}, f32[168,128]{1,0:T(8,128)S(1)}, f32[32,128]{1,0:T(8,128)S(1)}) custom-call(f32[168,128]{1,0:T(8,128)S(1)} %get-tuple-element.31.strip_x, f32[168,128]{1,0:T(8,128)S(1)} %get-tuple-element.32.strip_r, f32[168,128]{1,0:T(8,128)S(1)} %get-tuple-element.33.strip_c, f32[24,256]{1,0:T(8,128)S(1)} %collective-permute-done.2.a_ref, ...), custom_call_target="tpu_custom_call" | custom-call | flops 100000 | tf_op jit(solution)/shard_map/pallas_call | solution.py:374
  12.6 14.9 %all_to_all.11 = f32[32,1,128]{2,1,0:T(1,128)S(1)} all-to-all(f32[32,1,128]{2,1,0:T(1,128)S(1)} %bitcast.6), channel_id=1, replica_groups=mesh['bx'=4,'by'=8] {'bx','by'}, dimensions={0} | all-to-all | bytes 32768 | tf_op jit(solution)/shard_map/all_to_all | solution.py:381
  27.5 1.3 %shard_map.72 = (f32[152,256]{1,0:T(8,128)}, f32[152,256]{1,0:T(8,128)}, f32[1]{0:T(128)}) custom-call(f32[32,128]{1,0:T(8,128)S(1)} %bitcast.5, f32[152,256]{1,0:T(8,128)S(1)} %get-tuple-element.38.x_ref, f32[168,256]{1,0:T(8,128)S(1)} %get-tuple-element.39.r_ref, f32[152,128]{1,0:T(8,128)S(1)} %get-tuple-element.40.strip_x, ...), custom_call_target="tpu_custom_call" | custom-call | flops 100000 | tf_op jit(solution)/shard_map/pallas_call | solution.py:382
Async XLA Ops:
  1.5 2.7 %collective-permute-start = (f32[24,256]{1,0:T(8,128)S(1)}, f32[24,256]{1,0:T(8,128)S(1)}, u32[]{:S(2)}, u32[]{:S(2)}) collective-permute-start(f32[24,256]{1,0:T(8,128)S(1)} %get-tuple-element.27), channel_id=1, source_target_pairs={{0,1},{1,0},{2,3},{3,2},{4,5},{5,4},{6,7},{7,6},{8,9},{9,8},{10,11... | collective-permute-start | bytes 73736 | tf_op jit(solution)/shard_map/ppermute | solution.py:308
  2.1 2.1 %collective-permute-start.1 = (f32[24,256]{1,0:T(8,128)S(1)}, f32[24,256]{1,0:T(8,128)S(1)}, u32[]{:S(2)}, u32[]{:S(2)}) collective-permute-start(f32[24,256]{1,0:T(8,128)S(1)} %get-tuple-element.28), channel_id=1, source_target_pairs={{1,2},{2,1},{3,4},{4,3},{5,6},{6,5},{7,31},{9,10},{10,9},{11,12},{... | collective-permute-start | bytes 73736 | tf_op jit(solution)/shard_map/ppermute | solution.py:308
  4.4 5.7 %collective-permute-start.2 = (f32[24,256]{1,0:T(8,128)S(1)}, f32[24,256]{1,0:T(8,128)S(1)}, u32[]{:S(2)}, u32[]{:S(2)}) collective-permute-start(f32[24,256]{1,0:T(8,128)S(1)} %get-tuple-element.34), channel_id=1, source_target_pairs={{0,8},{1,9},{2,10},{3,11},{4,12},{5,13},{6,14},{7,15},{8,0},{9,1},... | collective-permute-start | bytes 73736 | tf_op jit(solution)/shard_map/ppermute | solution.py:308
  6.9 4.7 %collective-permute-start.3 = (f32[24,256]{1,0:T(8,128)S(1)}, f32[24,256]{1,0:T(8,128)S(1)}, u32[]{:S(2)}, u32[]{:S(2)}) collective-permute-start(f32[24,256]{1,0:T(8,128)S(1)} %get-tuple-element.35), channel_id=1, source_target_pairs={{0,24},{1,25},{2,26},{3,27},{4,28},{5,29},{6,30},{7,31},{8,16},{9,... | collective-permute-start | bytes 73736 | tf_op jit(solution)/shard_map/ppermute | solution.py:308

commit v5 on v4

--- a/solution.py
+++ b/solution.py
@@ -14,8 +14,10 @@
 SUB = 8
 LANE = 128
 FIELDS = 3
+DEPTH = ITERS + 1
+COLUMNS = 2 * SUB
+LEFT = LANE // 2 - SUB + DEPTH
 VMEM = pl.BlockSpec(memory_space=pltpu.VMEM)
-SMEM = pl.BlockSpec(memory_space=pltpu.SMEM)
 HBM = pl.BlockSpec(memory_space=pltpu.HBM)
 GRANT = pltpu.CompilerParams(vmem_limit_bytes=8 << 20)
 
@@ -73,13 +75,13 @@
     lane = lax.broadcasted_iota(jnp.int32, (rows, LANE), 1)
     packed = jnp.zeros((rows, LANE), jnp.float32)
     for f, field in enumerate(fields):
-        at = f * SUB
+        at = f * DEPTH
         left = field[:, :LANE]
         left = pltpu.roll(left, at, 1) if at else left
-        packed = jnp.where((lane >= at) & (lane < at + SUB), left, packed)
-        at = (FIELDS + f) * SUB
-        right = pltpu.roll(field[:, cols - LANE :], at + SUB, 1)
-        packed = jnp.where((lane >= at) & (lane < at + SUB), right, packed)
+        packed = jnp.where((lane >= at) & (lane < at + DEPTH), left, packed)
+        at = COLUMNS + f * DEPTH
+        right = pltpu.roll(field[:, cols - LANE :], at + DEPTH, 1)
+        packed = jnp.where((lane >= at) & (lane < at + DEPTH), right, packed)
     return packed
 
 
@@ -97,7 +99,7 @@
     packed = pack_columns(fields)
     width = columns_ref.shape[1]
     packed = jnp.concatenate([packed, jnp.zeros((width - packed.shape[0], LANE), jnp.float32)], axis=0)
-    columns_ref[...] = packed.T[: 2 * FIELDS * SUB]
+    columns_ref[...] = packed.T[: 2 * COLUMNS]
 
 
 def mirrored(tile):
@@ -110,7 +112,7 @@
     return jnp.concatenate(parts, axis=1)
 
 
-def halo_kernel(rows, near_ref, far_ref, columns_ref, halo_ref, a_ref, b_ref):
+def halo_kernel(rows, far_ref, near_ref, columns_ref, halo_ref, a_ref, b_ref):
     odd, odd_x = is_odd("by"), is_odd("bx")
     fold = lax.axis_index("by") == lax.axis_size("by") - 1
     n = FIELDS * SUB
@@ -130,22 +132,31 @@
     ]
     packed = pack_columns(fields)
     width = columns_ref.shape[1]
-    start = rows // LANE * LANE
+    start = width - LANE
     before, after = rows - start, width - rows - 2 * SUB
     pieces = [packed]
     if before:
         pieces.insert(0, jnp.zeros((before, LANE), jnp.float32))
     if after:
         pieces.append(jnp.zeros((after, LANE), jnp.float32))
-    ends = jnp.concatenate(pieces, axis=0).T[: 2 * n]
-    for at, first, second in ((slice(0, start), None, None), (slice(start, width), ends[:n], ends[n:])):
-        if at.stop == at.start:
-            continue
-        left, right = columns_ref[0:n, at], columns_ref[n : 2 * n, at]
-        if first is not None:
-            left, right = left + first, right + second
-        a_ref[:, at] = jnp.where(odd_x, left, right)
-        b_ref[:, at] = jnp.where(odd_x, right, left)
+    rest = columns_ref[:, start:width] + jnp.concatenate(pieces, axis=0).T[: 2 * COLUMNS]
+    sides = []
+    for at in (slice(0, COLUMNS), slice(COLUMNS, 2 * COLUMNS)):
+        parts = [columns_ref[at, p : p + LANE] for p in range(0, start, LANE)]
+        sides.append(jnp.concatenate(parts + [folded(rest[at])], axis=0))
+    a_ref[...] = jnp.where(odd_x, sides[0], sides[1])
+    b_ref[...] = jnp.where(odd_x, sides[1], sides[0])
+
+
+def folded(rest):
+    return rest[0:SUB] + pltpu.roll(rest[SUB:COLUMNS], LANE // 2, 1)
+
+
+def unfolded(value):
+    parts = [value[p : p + COLUMNS] for p in range(0, value.shape[0] - SUB, COLUMNS)]
+    rest = value[value.shape[0] - SUB :]
+    parts.append(jnp.concatenate([rest, pltpu.roll(rest, LANE // 2, 1)], axis=0))
+    return jnp.concatenate(parts, axis=1)
 
 
 def coefficients():
@@ -238,12 +249,12 @@
     high = d_s.shape[0]
     n = FIELDS * SUB
     lane = lax.broadcasted_iota(jnp.int32, (high, LANE), 1)
-    left, right = (lane >= LANE // 2) & (lane < LANE // 2 + 2 * SUB), lane >= LANE - 2 * SUB
+    left, right = (lane >= LEFT) & (lane < LEFT + 2 * SUB), lane >= LANE - 2 * SUB
     for f, (ref, main, strip) in enumerate(((d_s, x_ref, strip_x), (out_r_ref, f_ref, strip_r), (c_s, c_ref, strip_c))):
         ref[0:rows, :] = main[...]
         ref[rows : rows + SUB, :] = halo_ref[f * SUB : (f + 1) * SUB, :]
         ref[rows + SUB : high, :] = halo_ref[n + f * SUB : n + (f + 1) * SUB, :]
-        ends = jnp.where(left, pltpu.roll(ref[:, 0:LANE], LANE // 2, 1), 0.0)
+        ends = jnp.where(left, pltpu.roll(ref[:, 0:LANE], LEFT, 1), 0.0)
         strip[...] = jnp.where(right, ref[:, cols - LANE : cols], ends)
     column = lax.broadcasted_iota(jnp.int32, (SUB, cols), 1)
     weigh = (column >= SUB) & (column < cols - SUB)
@@ -252,38 +263,37 @@
     pair_ref[SUB : 2 * SUB, :] = jnp.broadcast_to(lower, (SUB, LANE))
 
 
-def strip_kernel(strip_x, strip_r, strip_c, a_ref, b_ref, pair_ref, out_x_ref, out_r_ref, pairs_ref, d_s, c_s):
+def strip_kernel(strip_x, strip_r, strip_c, b_ref, a_ref, pair_ref, out_x_ref, out_r_ref, pairs_ref, d_s, c_s):
     odd_x = is_odd("bx")
     high = d_s.shape[0]
-    n = FIELDS * SUB
-    middle = LANE // 2
-    a, b = a_ref[...], b_ref[...]
+    a, b = unfolded(a_ref[...]), unfolded(b_ref[...])
     left, right = jnp.where(odd_x, a, b), jnp.where(odd_x, b, a)
-    gap = jnp.zeros((middle - SUB - n, a.shape[1]), jnp.float32)
-    rest = jnp.zeros((middle + SUB - n, a.shape[1]), jnp.float32)
+    start = LEFT - DEPTH
+    gap = jnp.zeros((start - COLUMNS, a.shape[1]), jnp.float32)
+    rest = jnp.zeros((LANE - start - COLUMNS, a.shape[1]), jnp.float32)
     sides = jnp.concatenate([right, gap, left, rest], axis=0).T[0:high]
     lane = lax.broadcasted_iota(jnp.int32, (high, LANE), 1)
-    ghost = (lane < SUB) | ((lane >= middle - SUB) & (lane < middle))
+    ghost = (lane < DEPTH) | ((lane >= start) & (lane < LEFT))
     for f, (ref, strip) in enumerate(((d_s, strip_x), (out_r_ref, strip_r), (c_s, strip_c))):
-        side = pltpu.roll(sides, LANE - f * SUB, 1) if f else sides
+        side = pltpu.roll(sides, LANE - f * DEPTH, 1) if f else sides
         ref[...] = jnp.where(ghost, side, strip[...])
     lane = lax.broadcasted_iota(jnp.int32, (SUB, LANE), 1)
-    weigh = ((lane >= middle) & (lane < middle + SUB)) | (lane >= LANE - SUB)
+    weigh = ((lane >= LEFT) & (lane < LEFT + SUB)) | (lane >= LANE - SUB)
     ends = sweeps(out_x_ref.shape[0] // SUB, out_x_ref, d_s, out_r_ref, c_s, weigh)
     upper, lower = pair_add(ends, (pair_ref[0:SUB, :], pair_ref[SUB : 2 * SUB, :]))
-    tile = jnp.where(lane < middle, upper, lower)
+    tile = jnp.where(lane < LANE // 2, upper, lower)
     for i in range(pairs_ref.shape[0] // SUB):
         pairs_ref[i * SUB : (i + 1) * SUB, :] = tile
 
 
-def norm_kernel(cells, pairs_ref, x_ref, r_ref, strip_x, strip_r, x_hbm, r_hbm, norm_ref, x_s, r_s, sem):
+def norm_kernel(cells, pairs_ref, x_ref, r_ref, strip_x, strip_r, x_hbm, r_hbm, norm_hbm, x_s, r_s, norm_s, sem):
     rows, cols = x_s.shape
     lane = lax.broadcasted_iota(jnp.int32, (rows, LANE), 1)
     copies = []
     for i, (main, strip, joined, out) in enumerate(((x_ref, strip_x, x_s, x_hbm), (r_ref, strip_r, r_s, r_hbm))):
         joined[...] = main[0:rows, :]
         ends = strip[0:rows, :]
-        joined[:, 0:LANE] = jnp.where(lane < SUB, pltpu.roll(ends, LANE // 2, 1), joined[:, 0:LANE])
+        joined[:, 0:LANE] = jnp.where(lane < SUB, pltpu.roll(ends, LANE - LEFT, 1), joined[:, 0:LANE])
         joined[:, cols - LANE : cols] = jnp.where(lane >= LANE - SUB, ends, joined[:, cols - LANE : cols])
         copies.append(pltpu.make_async_copy(joined, out, sem.at[i]))
         copies[i].start()
@@ -292,7 +302,9 @@
         upper = pairs_ref[i * SUB : (i + 1) * SUB, :]
         pairs.append((upper, pltpu.roll(upper, LANE // 2, 1)))
     upper, lower = pair_total(pairs)
-    norm_ref[0] = jnp.sqrt((upper + lower) * (1.0 / cells))[0, 0]
+    norm_s[0] = jnp.sqrt((upper + lower) * (1.0 / cells))[0, 0]
+    copies.append(pltpu.make_async_copy(norm_s, norm_hbm, sem.at[2]))
+    copies[2].start()
     for copy in copies:
         copy.wait()
 
@@ -314,9 +326,11 @@
     devices = wide * high
     assert rows % SUB == 0 and cols % LANE == 0 and devices % SUB == 0
     assert wide % 2 == 0 and high % 2 == 0
+    assert rows % LANE + 2 * SUB <= LANE // 2 and FIELDS * DEPTH <= COLUMNS
     n = FIELDS * SUB
     tall = rows + 2 * SUB
-    span = -(-tall // LANE) * LANE
+    span = rows // LANE * LANE + LANE
+    packed = span // LANE * COLUMNS - SUB
     f32 = functools.partial(jax.ShapeDtypeStruct, dtype=jnp.float32)
     held = functools.partial(pltpu.VMEM, dtype=jnp.float32)
     fields = [pltpu.with_memory_space_constraint(v, pltpu.HBM) for v in (forcing, guess, shift, ocean)]
@@ -346,21 +360,21 @@
         return ((((b - 1) % wide) ^ 1) + 1) % wide, j
 
     shape = (wide, high)
+    far = swap(far, shape, next_chip)
     near = swap(near, shape, own_chip)
-    far = swap(far, shape, next_chip)
     x, f, c, columns = call(
         block_kernel,
-        (f32((rows, cols)),) * 3 + (f32((2 * n, span)),),
+        (f32((rows, cols)),) * 3 + (f32((2 * COLUMNS, span)),),
         [HBM] * 4,
         (VMEM,) * 4,
         [pltpu.VMEM((rows, cols), v.dtype) for v in fields] + [pltpu.SemaphoreType.DMA((4,))],
     )(*fields)
     halo, a, b = call(
         functools.partial(halo_kernel, rows),
-        (f32((2 * n, cols)), f32((n, span)), f32((n, span))),
+        (f32((2 * n, cols)),) + (f32((packed, LANE)),) * 2,
         [VMEM] * 3,
         (VMEM,) * 3,
-    )(near, far, columns)
+    )(far, near, columns)
     a = swap(a, shape, even_pair)
     b = swap(b, shape, odd_pair)
     high = (tall, LANE)
@@ -377,14 +391,14 @@
         [VMEM] * 6,
         (VMEM,) * 3,
         [pltpu.VMEM(high, jnp.float32)] * 2,
-    )(*strips, a, b, pair)
+    )(*strips, b, a, pair)
     pairs = lax.all_to_all(pairs, ("bx", "by"), 0, 0, tiled=True)
     x, r, norm = call(
         functools.partial(norm_kernel, rows * cols * devices),
         (f32((rows, cols)), f32((rows, cols)), f32((1,))),
         [VMEM] * 5,
-        (HBM, HBM, SMEM),
-        [pltpu.VMEM((rows, cols), jnp.float32)] * 2 + [pltpu.SemaphoreType.DMA((2,))],
+        (HBM,) * 3,
+        [pltpu.VMEM((rows, cols), jnp.float32)] * 2 + [pltpu.SMEM((1,), jnp.float32), pltpu.SemaphoreType.DMA((3,))],
     )(pairs, x, r, strip_x, strip_r)
     return (x, r, norm[0])
 

time: 29.1 us -> 27.8 us (0.955)
  blocking collectives: 14.9 us -> 11.3 us
  starting transfers between devices: 5.25 us -> 8.14 us
  Pallas kernels: 6.48 us -> 5.94 us
    all_to_all x1, blocking collectives: 14.9 us -> 11.3 us  [per_device(): pairs = lax.all_to_all(pairs, ('bx', 'by'), 0, 0, tiled=True)]
    ppermute x4, starting transfers between devices: 5.25 us -> 8.14 us  [swap(): return lax.ppermute(value, ('bx', 'by'), moves)]
    pallas_call x1, Pallas kernels: 1.35 us -> 0.85 us  [per_device(): call(functools.partial(norm_kernel, rows * cols * devices), (f32((rows, c...]
where the time goes in v5:
time: 27.8 us; the launch traced here: 27.6 us
  blocking collectives  11.3 us (41%)
  starting transfers between devices  8.14 us (29%)
  Pallas kernels  5.94 us (21%)
  waiting for transfers between devices  1.5 us (5%)
  between operations  0.67 us (2%)
    all_to_all x1, blocking collectives, per_device(): pairs = lax.all_to_all(pairs, ('bx', 'by'), 0, 0, tiled=True)  11.3 us
    ppermute x4, starting transfers between devices, swap(): return lax.ppermute(value, ('bx', 'by'), moves)  8.14 us
    pallas_call x1, Pallas kernels, per_device(): call(interior_kernel, (held((rows, cols)), held((tall, cols)), held((2 *...  1.67 us
    ppermute x4, waiting for transfers between devices, swap(): return lax.ppermute(value, ('bx', 'by'), moves)  1.5 us
    pallas_call x1, Pallas kernels, per_device(): call(block_kernel, (f32((rows, cols)),) * 3 + (f32((2 * COLUMNS, span)),)...  1.42 us
    pallas_call x1, Pallas kernels, per_device(): call(strip_kernel, (held((rows, LANE)), held(high), held((devices, LANE))...  0.9 us
    pallas_call x1, Pallas kernels, per_device(): call(edge_kernel, (f32((n, cols)),) * 2, [HBM] * 4, (VMEM,) * 2, edges *...  0.89 us
    pallas_call x1, Pallas kernels, per_device(): call(functools.partial(norm_kernel, rows * cols * devices), (f32((rows, c...  0.85 us
  transfers between devices with their start and end apart: 4, of which 1 were waited for; matrix products, arithmetic and copies ran while one was open for 0% of the time, Pallas kernels for 11%

profile of v5, /device:TPU:0, one launch (start us, length us, event | category | flops | bytes accessed | tf_op | source)
XLA Modules:
  0.0 27.6 jit_solution(14338787875232269145)
XLA Ops:
  0.6 0.9 %shard_map.68 = (f32[24,256]{1,0:T(8,128)S(1)}, f32[24,256]{1,0:T(8,128)S(1)}) custom-call(f32[152,256]{1,0:T(8,128)} %refs_0_.3, f32[152,256]{1,0:T(8,128)} %refs_1_.3, f32[152,256]{1,0:T(8,128)} %refs_2_.3, s32[152,256]{1,0:T(8,128)} %refs_3_.3), custom_call_target="tpu_custom_call" | custom-call | flops 100000 | tf_op jit(solution)/shard_map/pallas_call | solution.py:338
  1.5 0.7 %collective-permute-start = (f32[24,256]{1,0:T(8,128)S(1)}, f32[24,256]{1,0:T(8,128)S(1)}, u32[]{:S(2)}, u32[]{:S(2)}) collective-permute-start(f32[24,256]{1,0:T(8,128)S(1)} %get-tuple-element.27), channel_id=1, source_target_pairs={{1,2},{2,1},{3,4},{4,3},{5,6},{6,5},{7,31},{9,10},{10,9},{11,12},{... | collective-permute-start | bytes 73736 | tf_op jit(solution)/shard_map/ppermute | solution.py:320
  2.2 4.5 %collective-permute-start.1 = (f32[24,256]{1,0:T(8,128)S(1)}, f32[24,256]{1,0:T(8,128)S(1)}, u32[]{:S(2)}, u32[]{:S(2)}) collective-permute-start(f32[24,256]{1,0:T(8,128)S(1)} %get-tuple-element.28), channel_id=1, source_target_pairs={{0,1},{1,0},{2,3},{3,2},{4,5},{5,4},{6,7},{7,6},{8,9},{9,8},{10,11... | collective-permute-start | bytes 73736 | tf_op jit(solution)/shard_map/ppermute | solution.py:320
  6.7 1.4 %shard_map.67 = (f32[152,256]{1,0:T(8,128)S(1)}, f32[152,256]{1,0:T(8,128)S(1)}, f32[152,256]{1,0:T(8,128)S(1)}, f32[32,256]{1,0:T(8,128)S(1)}) custom-call(f32[152,256]{1,0:T(8,128)} %refs_0_.3, f32[152,256]{1,0:T(8,128)} %refs_1_.3, f32[152,256]{1,0:T(8,128)} %refs_2_.3, s32[152,256]{1,0:T(8,128)} %refs_3_.3), custom_call_target="tpu_custom_call" | custom-call | flops 100000 | tf_op jit(solution)/shard_map/pallas_call | solution.py:365
  8.1 0.0 collective-permute-done.far_ref
  8.1 0.0 collective-permute-done.1.near_ref
  8.1 0.2 shard_map.69
  8.3 2.5 %collective-permute-start.2 = (f32[24,128]{1,0:T(8,128)S(1)}, f32[24,128]{1,0:T(8,128)S(1)}, u32[]{:S(2)}, u32[]{:S(2)}) collective-permute-start(f32[24,128]{1,0:T(8,128)S(1)} %get-tuple-element.34), channel_id=1, source_target_pairs={{0,24},{1,25},{2,26},{3,27},{4,28},{5,29},{6,30},{7,31},{8,16},{9,... | collective-permute-start | bytes 36872 | tf_op jit(solution)/shard_map/ppermute | solution.py:320
  10.8 0.5 %collective-permute-start.3 = (f32[24,128]{1,0:T(8,128)S(1)}, f32[24,128]{1,0:T(8,128)S(1)}, u32[]{:S(2)}, u32[]{:S(2)}) collective-permute-start(f32[24,128]{1,0:T(8,128)S(1)} %get-tuple-element.35), channel_id=1, source_target_pairs={{0,8},{1,9},{2,10},{3,11},{4,12},{5,13},{6,14},{7,15},{8,0},{9,1},... | collective-permute-start | bytes 36872 | tf_op jit(solution)/shard_map/ppermute | solution.py:320
  11.4 1.7 %shard_map.70 = (f32[152,256]{1,0:T(8,128)S(1)}, f32[168,256]{1,0:T(8,128)S(1)}, f32[16,128]{1,0:T(8,128)S(1)}, f32[168,128]{1,0:T(8,128)S(1)}, f32[168,128]{1,0:T(8,128)S(1)}, /*index=5*/f32[168,128]{1,0:T(8,128)S(1)}) custom-call(f32[152,256]{1,0:T(8,128)S(1)} %get-tuple-element.24.x_ref, f32[152,256]{1,0:T(8,128)S(1)} %get-tuple-element.25.f_ref, ...), custom_call_target="tpu_custom_call" | custom-call | flops 100000 | tf_op jit(solution)/shard_map/pallas_call | solution.py:381
  13.0 0.0 collective-permute-done.2.b_ref
  13.0 1.5 %collective-permute-done.3.a_ref = f32[24,128]{1,0:T(8,128)S(1)} collective-permute-done((f32[24,128]{1,0:T(8,128)S(1)}, f32[24,128]{1,0:T(8,128)S(1)}, u32[]{:S(2)}, u32[]{:S(2)}) %collective-permute-start.3) | collective-permute-done | bytes 12320 | tf_op jit(solution)/shard_map/ppermute | solution.py:320
  14.5 0.9 %shard_map.71 = (f32[152,128]{1,0:T(8,128)S(1)}, f32[168,128]{1,0:T(8,128)S(1)}, f32[32,128]{1,0:T(8,128)S(1)}) custom-call(f32[168,128]{1,0:T(8,128)S(1)} %get-tuple-element.31.strip_x, f32[168,128]{1,0:T(8,128)S(1)} %get-tuple-element.32.strip_r, f32[168,128]{1,0:T(8,128)S(1)} %get-tuple-element.33.strip_c, f32[24,128]{1,0:T(8,128)S(1)} %collective-permute-done.2.b_ref, ...), custom_call_target="tpu_custom_call" | custom-call | flops 100000 | tf_op jit(solution)/shard_map/pallas_call | solution.py:388
  15.4 11.3 %all_to_all.11 = f32[32,1,128]{2,1,0:T(1,128)S(1)} all-to-all(f32[32,1,128]{2,1,0:T(1,128)S(1)} %bitcast.6), channel_id=1, replica_groups=mesh['bx'=4,'by'=8] {'bx','by'}, dimensions={0} | all-to-all | bytes 32768 | tf_op jit(solution)/shard_map/all_to_all | solution.py:395
  26.7 0.8 %shard_map.72 = (f32[152,256]{1,0:T(8,128)}, f32[152,256]{1,0:T(8,128)}, f32[1]{0:T(128)}) custom-call(f32[32,128]{1,0:T(8,128)S(1)} %bitcast.5, f32[152,256]{1,0:T(8,128)S(1)} %get-tuple-element.38.x_ref, f32[168,256]{1,0:T(8,128)S(1)} %get-tuple-element.39.r_ref, f32[152,128]{1,0:T(8,128)S(1)} %get-tuple-element.40.strip_x, ...), custom_call_target="tpu_custom_call" | custom-call | flops 100000 | tf_op jit(solution)/shard_map/pallas_call | solution.py:396
Async XLA Ops:
  1.5 6.6 %collective-permute-start = (f32[24,256]{1,0:T(8,128)S(1)}, f32[24,256]{1,0:T(8,128)S(1)}, u32[]{:S(2)}, u32[]{:S(2)}) collective-permute-start(f32[24,256]{1,0:T(8,128)S(1)} %get-tuple-element.27), channel_id=1, source_target_pairs={{1,2},{2,1},{3,4},{4,3},{5,6},{6,5},{7,31},{9,10},{10,9},{11,12},{... | collective-permute-start | bytes 73736 | tf_op jit(solution)/shard_map/ppermute | solution.py:320
  2.2 5.9 %collective-permute-start.1 = (f32[24,256]{1,0:T(8,128)S(1)}, f32[24,256]{1,0:T(8,128)S(1)}, u32[]{:S(2)}, u32[]{:S(2)}) collective-permute-start(f32[24,256]{1,0:T(8,128)S(1)} %get-tuple-element.28), channel_id=1, source_target_pairs={{0,1},{1,0},{2,3},{3,2},{4,5},{5,4},{6,7},{7,6},{8,9},{9,8},{10,11... | collective-permute-start | bytes 73736 | tf_op jit(solution)/shard_map/ppermute | solution.py:320
  8.3 4.7 %collective-permute-start.2 = (f32[24,128]{1,0:T(8,128)S(1)}, f32[24,128]{1,0:T(8,128)S(1)}, u32[]{:S(2)}, u32[]{:S(2)}) collective-permute-start(f32[24,128]{1,0:T(8,128)S(1)} %get-tuple-element.34), channel_id=1, source_target_pairs={{0,24},{1,25},{2,26},{3,27},{4,28},{5,29},{6,30},{7,31},{8,16},{9,... | collective-permute-start | bytes 36872 | tf_op jit(solution)/shard_map/ppermute | solution.py:320
  10.8 3.7 %collective-permute-start.3 = (f32[24,128]{1,0:T(8,128)S(1)}, f32[24,128]{1,0:T(8,128)S(1)}, u32[]{:S(2)}, u32[]{:S(2)}) collective-permute-start(f32[24,128]{1,0:T(8,128)S(1)} %get-tuple-element.35), channel_id=1, source_target_pairs={{0,8},{1,9},{2,10},{3,11},{4,12},{5,13},{6,14},{7,15},{8,0},{9,1},... | collective-permute-start | bytes 36872 | tf_op jit(solution)/shard_map/ppermute | solution.py:320

commit v6 on v5

--- a/solution.py
+++ b/solution.py
@@ -118,7 +118,7 @@
     n = FIELDS * SUB
     near, far = near_ref[...], far_ref[...]
     halo_ref[0:n, :] = jnp.where(odd, far, near)
-    halo_ref[n : 2 * n, :] = jnp.where(odd, near, far)
+    halo_ref[n : 2 * n, :] = jnp.where(lax.axis_index("by") == 0, 0.0, jnp.where(odd, near, far))
 
     @pl.when(fold)
     def _():
@@ -175,11 +175,13 @@
 def pair_add(first, second):
     total = first[0] + second[0]
     backed = total - first[0]
-    error = first[0] - (total - backed) + (second[0] - backed)
-    error = error + first[1] + second[1]
-    upper = total + error
-    lower = error - (upper - total)
-    return (upper, lower)
+    error = (first[0] - (total - backed)) + (second[0] - backed)
+    return (total, (first[1] + second[1]) + error)
+
+
+def settled(pair):
+    upper = pair[0] + pair[1]
+    return (upper, pair[1] - (upper - pair[0]))
 
 
 def pair_tree(pairs):
@@ -280,7 +282,7 @@
     lane = lax.broadcasted_iota(jnp.int32, (SUB, LANE), 1)
     weigh = ((lane >= LEFT) & (lane < LEFT + SUB)) | (lane >= LANE - SUB)
     ends = sweeps(out_x_ref.shape[0] // SUB, out_x_ref, d_s, out_r_ref, c_s, weigh)
-    upper, lower = pair_add(ends, (pair_ref[0:SUB, :], pair_ref[SUB : 2 * SUB, :]))
+    upper, lower = settled(pair_add(ends, (pair_ref[0:SUB, :], pair_ref[SUB : 2 * SUB, :])))
     tile = jnp.where(lane < LANE // 2, upper, lower)
     for i in range(pairs_ref.shape[0] // SUB):
         pairs_ref[i * SUB : (i + 1) * SUB, :] = tile
@@ -301,7 +303,7 @@
     for i in range(pairs_ref.shape[0] // SUB):
         upper = pairs_ref[i * SUB : (i + 1) * SUB, :]
         pairs.append((upper, pltpu.roll(upper, LANE // 2, 1)))
-    upper, lower = pair_total(pairs)
+    upper, lower = settled(pair_total(pairs))
     norm_s[0] = jnp.sqrt((upper + lower) * (1.0 / cells))[0, 0]
     copies.append(pltpu.make_async_copy(norm_s, norm_hbm, sem.at[2]))
     copies[2].start()
@@ -348,7 +350,7 @@
 
     def next_chip(b, j):
         if j == 0:
-            return None
+            return (b ^ 1, j)
         if j == high - 1:
             return (wide - 1 - b, j)
         return (b, ((j - 1) ^ 1) + 1)

time: 27.8 us -> 26 us (0.935)
  starting transfers between devices: 8.14 us -> 6.76 us
  blocking collectives: 11.3 us -> 10.7 us
    ppermute x4, starting transfers between devices: 8.14 us -> 6.76 us  [swap(): return lax.ppermute(value, ('bx', 'by'), moves)]
    all_to_all x1, blocking collectives: 11.3 us -> 10.7 us  [per_device(): pairs = lax.all_to_all(pairs, ('bx', 'by'), 0, 0, tiled=True)]
  transfers between devices with their start and end apart: 4 -> 4, of which waited for: 1 -> 2; matrix products, arithmetic and copies ran while one was open for 0% -> 0% of each run, Pallas kernels for 11% -> 12%
where the time goes in v6:
time: 26 us; the launch traced here: 25.7 us
  blocking collectives  10.7 us (41%)
  starting transfers between devices  6.76 us (26%)
  Pallas kernels  5.94 us (23%)
  waiting for transfers between devices  1.63 us (6%)
  between operations  0.65 us (2%)
    all_to_all x1, blocking collectives, per_device(): pairs = lax.all_to_all(pairs, ('bx', 'by'), 0, 0, tiled=True)  10.7 us
    ppermute x4, starting transfers between devices, swap(): return lax.ppermute(value, ('bx', 'by'), moves)  6.76 us
    pallas_call x1, Pallas kernels, per_device(): call(interior_kernel, (held((rows, cols)), held((tall, cols)), held((2 *...  1.71 us
    ppermute x4, waiting for transfers between devices, swap(): return lax.ppermute(value, ('bx', 'by'), moves)  1.63 us
    pallas_call x1, Pallas kernels, per_device(): call(block_kernel, (f32((rows, cols)),) * 3 + (f32((2 * COLUMNS, span)),)...  1.42 us
    pallas_call x1, Pallas kernels, per_device(): call(edge_kernel, (f32((n, cols)),) * 2, [HBM] * 4, (VMEM,) * 2, edges *...  0.89 us
    pallas_call x1, Pallas kernels, per_device(): call(strip_kernel, (held((rows, LANE)), held(high), held((devices, LANE))...  0.86 us
    pallas_call x1, Pallas kernels, per_device(): call(functools.partial(norm_kernel, rows * cols * devices), (f32((rows, c...  0.85 us
  transfers between devices with their start and end apart: 4, of which 2 were waited for; matrix products, arithmetic and copies ran while one was open for 0% of the time, Pallas kernels for 12%

profile of v6, /device:TPU:0, one launch (start us, length us, event | category | flops | bytes accessed | tf_op | source)
XLA Modules:
  0.0 25.7 jit_solution(2406533079695903528)
XLA Ops:
  0.6 0.9 %shard_map.68 = (f32[24,256]{1,0:T(8,128)S(1)}, f32[24,256]{1,0:T(8,128)S(1)}) custom-call(f32[152,256]{1,0:T(8,128)} %refs_0_.3, f32[152,256]{1,0:T(8,128)} %refs_1_.3, f32[152,256]{1,0:T(8,128)} %refs_2_.3, s32[152,256]{1,0:T(8,128)} %refs_3_.3), custom_call_target="tpu_custom_call" | custom-call | flops 100000 | tf_op jit(solution)/shard_map/pallas_call | solution.py:340
  1.5 3.0 %collective-permute-start = (f32[24,256]{1,0:T(8,128)S(1)}, f32[24,256]{1,0:T(8,128)S(1)}, u32[]{:S(2)}, u32[]{:S(2)}) collective-permute-start(f32[24,256]{1,0:T(8,128)S(1)} %get-tuple-element.27), channel_id=1, source_target_pairs={{0,8},{1,2},{2,1},{3,4},{4,3},{5,6},{6,5},{7,31},{8,0},{9,10},{10,... | collective-permute-start | bytes 73736 | tf_op jit(solution)/shard_map/ppermute | solution.py:322
  4.6 0.2 collective-permute-start.1
  4.8 1.4 %shard_map.67 = (f32[152,256]{1,0:T(8,128)S(1)}, f32[152,256]{1,0:T(8,128)S(1)}, f32[152,256]{1,0:T(8,128)S(1)}, f32[32,256]{1,0:T(8,128)S(1)}) custom-call(f32[152,256]{1,0:T(8,128)} %refs_0_.3, f32[152,256]{1,0:T(8,128)} %refs_1_.3, f32[152,256]{1,0:T(8,128)} %refs_2_.3, s32[152,256]{1,0:T(8,128)} %refs_3_.3), custom_call_target="tpu_custom_call" | custom-call | flops 100000 | tf_op jit(solution)/shard_map/pallas_call | solution.py:367
  6.2 0.2 collective-permute-done.far_ref
  6.4 0.0 collective-permute-done.1.near_ref
  6.4 0.2 shard_map.69
  6.6 3.0 %collective-permute-start.2 = (f32[24,128]{1,0:T(8,128)S(1)}, f32[24,128]{1,0:T(8,128)S(1)}, u32[]{:S(2)}, u32[]{:S(2)}) collective-permute-start(f32[24,128]{1,0:T(8,128)S(1)} %get-tuple-element.34), channel_id=1, source_target_pairs={{0,24},{1,25},{2,26},{3,27},{4,28},{5,29},{6,30},{7,31},{8,16},{9,... | collective-permute-start | bytes 36872 | tf_op jit(solution)/shard_map/ppermute | solution.py:322
  9.6 0.5 %collective-permute-start.3 = (f32[24,128]{1,0:T(8,128)S(1)}, f32[24,128]{1,0:T(8,128)S(1)}, u32[]{:S(2)}, u32[]{:S(2)}) collective-permute-start(f32[24,128]{1,0:T(8,128)S(1)} %get-tuple-element.35), channel_id=1, source_target_pairs={{0,8},{1,9},{2,10},{3,11},{4,12},{5,13},{6,14},{7,15},{8,0},{9,1},... | collective-permute-start | bytes 36872 | tf_op jit(solution)/shard_map/ppermute | solution.py:322
  10.1 1.7 %shard_map.70 = (f32[152,256]{1,0:T(8,128)S(1)}, f32[168,256]{1,0:T(8,128)S(1)}, f32[16,128]{1,0:T(8,128)S(1)}, f32[168,128]{1,0:T(8,128)S(1)}, f32[168,128]{1,0:T(8,128)S(1)}, /*index=5*/f32[168,128]{1,0:T(8,128)S(1)}) custom-call(f32[152,256]{1,0:T(8,128)S(1)} %get-tuple-element.24.x_ref, f32[152,256]{1,0:T(8,128)S(1)} %get-tuple-element.25.f_ref, ...), custom_call_target="tpu_custom_call" | custom-call | flops 100000 | tf_op jit(solution)/shard_map/pallas_call | solution.py:383
  11.8 0.0 collective-permute-done.2.b_ref
  11.8 1.4 %collective-permute-done.3.a_ref = f32[24,128]{1,0:T(8,128)S(1)} collective-permute-done((f32[24,128]{1,0:T(8,128)S(1)}, f32[24,128]{1,0:T(8,128)S(1)}, u32[]{:S(2)}, u32[]{:S(2)}) %collective-permute-start.3) | collective-permute-done | bytes 12320 | tf_op jit(solution)/shard_map/ppermute | solution.py:322
  13.3 0.9 %shard_map.71 = (f32[152,128]{1,0:T(8,128)S(1)}, f32[168,128]{1,0:T(8,128)S(1)}, f32[32,128]{1,0:T(8,128)S(1)}) custom-call(f32[168,128]{1,0:T(8,128)S(1)} %get-tuple-element.31.strip_x, f32[168,128]{1,0:T(8,128)S(1)} %get-tuple-element.32.strip_r, f32[168,128]{1,0:T(8,128)S(1)} %get-tuple-element.33.strip_c, f32[24,128]{1,0:T(8,128)S(1)} %collective-permute-done.2.b_ref, ...), custom_call_target="tpu_custom_call" | custom-call | flops 100000 | tf_op jit(solution)/shard_map/pallas_call | solution.py:390
  14.1 10.7 %all_to_all.11 = f32[32,1,128]{2,1,0:T(1,128)S(1)} all-to-all(f32[32,1,128]{2,1,0:T(1,128)S(1)} %bitcast.6), channel_id=1, replica_groups=mesh['bx'=4,'by'=8] {'bx','by'}, dimensions={0} | all-to-all | bytes 32768 | tf_op jit(solution)/shard_map/all_to_all | solution.py:397
  24.8 0.8 %shard_map.72 = (f32[152,256]{1,0:T(8,128)}, f32[152,256]{1,0:T(8,128)}, f32[1]{0:T(128)}) custom-call(f32[32,128]{1,0:T(8,128)S(1)} %bitcast.5, f32[152,256]{1,0:T(8,128)S(1)} %get-tuple-element.38.x_ref, f32[168,256]{1,0:T(8,128)S(1)} %get-tuple-element.39.r_ref, f32[152,128]{1,0:T(8,128)S(1)} %get-tuple-element.40.strip_x, ...), custom_call_target="tpu_custom_call" | custom-call | flops 100000 | tf_op jit(solution)/shard_map/pallas_call | solution.py:398
Async XLA Ops:
  1.5 4.8 %collective-permute-start = (f32[24,256]{1,0:T(8,128)S(1)}, f32[24,256]{1,0:T(8,128)S(1)}, u32[]{:S(2)}, u32[]{:S(2)}) collective-permute-start(f32[24,256]{1,0:T(8,128)S(1)} %get-tuple-element.27), channel_id=1, source_target_pairs={{0,8},{1,2},{2,1},{3,4},{4,3},{5,6},{6,5},{7,31},{8,0},{9,10},{10,... | collective-permute-start | bytes 73736 | tf_op jit(solution)/shard_map/ppermute | solution.py:322
  4.6 1.8 %collective-permute-start.1 = (f32[24,256]{1,0:T(8,128)S(1)}, f32[24,256]{1,0:T(8,128)S(1)}, u32[]{:S(2)}, u32[]{:S(2)}) collective-permute-start(f32[24,256]{1,0:T(8,128)S(1)} %get-tuple-element.28), channel_id=1, source_target_pairs={{0,1},{1,0},{2,3},{3,2},{4,5},{5,4},{6,7},{7,6},{8,9},{9,8},{10,11... | collective-permute-start | bytes 73736 | tf_op jit(solution)/shard_map/ppermute | solution.py:322
  6.6 5.2 %collective-permute-start.2 = (f32[24,128]{1,0:T(8,128)S(1)}, f32[24,128]{1,0:T(8,128)S(1)}, u32[]{:S(2)}, u32[]{:S(2)}) collective-permute-start(f32[24,128]{1,0:T(8,128)S(1)} %get-tuple-element.34), channel_id=1, source_target_pairs={{0,24},{1,25},{2,26},{3,27},{4,28},{5,29},{6,30},{7,31},{8,16},{9,... | collective-permute-start | bytes 36872 | tf_op jit(solution)/shard_map/ppermute | solution.py:322
  9.6 3.7 %collective-permute-start.3 = (f32[24,128]{1,0:T(8,128)S(1)}, f32[24,128]{1,0:T(8,128)S(1)}, u32[]{:S(2)}, u32[]{:S(2)}) collective-permute-start(f32[24,128]{1,0:T(8,128)S(1)} %get-tuple-element.35), channel_id=1, source_target_pairs={{0,8},{1,9},{2,10},{3,11},{4,12},{5,13},{6,14},{7,15},{8,0},{9,1},... | collective-permute-start | bytes 36872 | tf_op jit(solution)/shard_map/ppermute | solution.py:322

commit v7 on v6

--- a/solution.py
+++ b/solution.py
@@ -70,19 +70,22 @@
         far_ref[at, :] = jnp.where(odd, top[f], low[f])
 
 
-def pack_columns(fields):
-    rows, cols = fields[0].shape
-    lane = lax.broadcasted_iota(jnp.int32, (rows, LANE), 1)
-    packed = jnp.zeros((rows, LANE), jnp.float32)
+def place(index):
+    per = LANE // COLUMNS
+    return index // per * SUB, index % per * COLUMNS
+
+
+def end_columns(fields, lane, index):
+    zero = jnp.zeros((SUB, LANE), jnp.float32)
+    left, right = zero, zero
     for f, field in enumerate(fields):
-        at = f * DEPTH
-        left = field[:, :LANE]
-        left = pltpu.roll(left, at, 1) if at else left
-        packed = jnp.where((lane >= at) & (lane < at + DEPTH), left, packed)
-        at = COLUMNS + f * DEPTH
-        right = pltpu.roll(field[:, cols - LANE :], at + DEPTH, 1)
-        packed = jnp.where((lane >= at) & (lane < at + DEPTH), right, packed)
-    return packed
+        at = place(index)[1] + f * DEPTH
+        first, last = field[:, :LANE], field[:, field.shape[1] - LANE :]
+        left = jnp.where((lane >= at) & (lane < at + DEPTH), pltpu.roll(first, at, 1) if at else first, left)
+        at = (at + LEFT - DEPTH) % LANE
+        here = (lane >= at) & (lane < at + DEPTH) | (lane < at + DEPTH - LANE)
+        right = jnp.where(here, pltpu.roll(last, (at + DEPTH) % LANE, 1), right)
+    return left, right
 
 
 def block_kernel(*refs):
@@ -96,10 +99,17 @@
     fields = masked_fields(*(ref[...] for ref in held))
     for ref, field in zip((x_ref, r_ref, c_ref), fields):
         ref[...] = field
-    packed = pack_columns(fields)
-    width = columns_ref.shape[1]
-    packed = jnp.concatenate([packed, jnp.zeros((width - packed.shape[0], LANE), jnp.float32)], axis=0)
-    columns_ref[...] = packed.T[: 2 * COLUMNS]
+    lane = lax.broadcasted_iota(jnp.int32, (SUB, LANE), 1)
+    half = columns_ref.shape[0] // 2
+    sums = {}
+    for t in range(x_ref.shape[0] // SUB):
+        ends = end_columns([field[t * SUB : (t + 1) * SUB] for field in fields], lane, t)
+        row = place(t)[0]
+        sums[row] = [p + q for p, q in zip(sums[row], ends)] if row in sums else ends
+    for row in range(0, half, SUB):
+        left, right = sums.get(row, [jnp.zeros((SUB, LANE), jnp.float32)] * 2)
+        columns_ref[row : row + SUB, :] = left
+        columns_ref[half + row : half + row + SUB, :] = right
 
 
 def mirrored(tile):
@@ -126,37 +136,19 @@
             at = slice(f * SUB, (f + 1) * SUB)
             halo_ref[at, :] = mirrored(halo_ref[at, :])
 
-    fields = [
-        jnp.concatenate([halo_ref[f * SUB : (f + 1) * SUB, :], halo_ref[n + f * SUB : n + (f + 1) * SUB, :]], axis=0)
-        for f in range(FIELDS)
-    ]
-    packed = pack_columns(fields)
-    width = columns_ref.shape[1]
-    start = width - LANE
-    before, after = rows - start, width - rows - 2 * SUB
-    pieces = [packed]
-    if before:
-        pieces.insert(0, jnp.zeros((before, LANE), jnp.float32))
-    if after:
-        pieces.append(jnp.zeros((after, LANE), jnp.float32))
-    rest = columns_ref[:, start:width] + jnp.concatenate(pieces, axis=0).T[: 2 * COLUMNS]
-    sides = []
-    for at in (slice(0, COLUMNS), slice(COLUMNS, 2 * COLUMNS)):
-        parts = [columns_ref[at, p : p + LANE] for p in range(0, start, LANE)]
-        sides.append(jnp.concatenate(parts + [folded(rest[at])], axis=0))
-    a_ref[...] = jnp.where(odd_x, sides[0], sides[1])
-    b_ref[...] = jnp.where(odd_x, sides[1], sides[0])
-
-
-def folded(rest):
-    return rest[0:SUB] + pltpu.roll(rest[SUB:COLUMNS], LANE // 2, 1)
-
-
-def unfolded(value):
-    parts = [value[p : p + COLUMNS] for p in range(0, value.shape[0] - SUB, COLUMNS)]
-    rest = value[value.shape[0] - SUB :]
-    parts.append(jnp.concatenate([rest, pltpu.roll(rest, LANE // 2, 1)], axis=0))
-    return jnp.concatenate(parts, axis=1)
+    lane = lax.broadcasted_iota(jnp.int32, (SUB, LANE), 1)
+    half = a_ref.shape[0]
+    left = [columns_ref[p : p + SUB, :] for p in range(0, half, SUB)]
+    right = [columns_ref[half + p : half + p + SUB, :] for p in range(0, half, SUB)]
+    for i in range(2):
+        fields = [halo_ref[i * n + f * SUB : i * n + (f + 1) * SUB, :] for f in range(FIELDS)]
+        first, last = end_columns(fields, lane, rows // SUB + i)
+        g = place(rows // SUB + i)[0] // SUB
+        left[g], right[g] = left[g] + first, right[g] + last
+    for g in range(half // SUB):
+        at = slice(g * SUB, (g + 1) * SUB)
+        a_ref[at, :] = jnp.where(odd_x, left[g], right[g])
+        b_ref[at, :] = jnp.where(odd_x, right[g], left[g])
 
 
 def coefficients():
@@ -246,6 +238,57 @@
     return pair_total([(q, zero) for q in squares])
 
 
+def staggered(inner, x_s, d_s, r_s, c_s, weigh, lag):
+    tall, wide = d_s.shape
+    tiles = tall // SUB
+    theta, steps = coefficients()
+    row_id = lax.broadcasted_iota(jnp.int32, (SUB, wide), 0)
+    first_row, last_row = row_id == 0, row_id == SUB - 1
+    order = [tiles - 1] + list(range(tiles - 1))
+
+    def across(v):
+        pair = pltpu.roll(v, 1, 1) + pltpu.roll(v, wide - 1, 1)
+        mixed = v + 0.5 * pair
+        return v, pair, pltpu.roll(mixed, 1, 0), pltpu.roll(mixed, SUB - 1, 0)
+
+    squares = []
+    held = [{} for _ in range(ITERS + 1)]
+    for step in range(tiles + 1 + lag * ITERS):
+        if step < tiles:
+            at = order[step] * SUB
+            held[0][step] = across(d_s[at : at + SUB, :])
+        for sweep in range(ITERS + 1):
+            p = step - 1 - lag * sweep
+            if not 0 <= p < tiles:
+                continue
+            v, pair, down, up = held[sweep][p]
+            before, after = held[sweep].pop(p - 1, None), held[sweep].get(p + 1)
+            main = order[p] < inner
+            if sweep == ITERS and not main:
+                continue
+            from_below = down if before is None else jnp.where(first_row, before[2], down)
+            from_above = up if after is None else jnp.where(last_row, after[3], up)
+            at = slice(order[p] * SUB, (order[p] + 1) * SUB)
+            c = c_s[at, :]
+            image = jnp.where(c > 0.0, c * v - (pair + (from_below + from_above)), jnp.zeros_like(c))
+            r = r_s[at, :] - image
+            r_s[at, :] = r
+            if sweep < ITERS:
+                if sweep == 0:
+                    d = r * (1.0 / theta)
+                else:
+                    keep, gain = steps[sweep - 1]
+                    d = keep * v + gain * r
+                held[sweep + 1][p] = across(d)
+                if main:
+                    x_s[at, :] = (v if sweep == 0 else x_s[at, :]) + d
+            else:
+                r = jnp.where(weigh, r, jnp.zeros_like(r))
+                squares.append(jnp.sum(r * r, axis=1, keepdims=True))
+    zero = jnp.zeros_like(squares[0])
+    return pair_total([(q, zero) for q in squares])
+
+
 def interior_kernel(x_ref, f_ref, c_ref, halo_ref, out_x_ref, out_r_ref, pair_ref, strip_x, strip_r, strip_c, d_s, c_s):
     rows, cols = x_ref.shape
     high = d_s.shape[0]
@@ -268,20 +311,22 @@
 def strip_kernel(strip_x, strip_r, strip_c, b_ref, a_ref, pair_ref, out_x_ref, out_r_ref, pairs_ref, d_s, c_s):
     odd_x = is_odd("bx")
     high = d_s.shape[0]
-    a, b = unfolded(a_ref[...]), unfolded(b_ref[...])
+    a, b = a_ref[...], b_ref[...]
     left, right = jnp.where(odd_x, a, b), jnp.where(odd_x, b, a)
     start = LEFT - DEPTH
-    gap = jnp.zeros((start - COLUMNS, a.shape[1]), jnp.float32)
-    rest = jnp.zeros((LANE - start - COLUMNS, a.shape[1]), jnp.float32)
-    sides = jnp.concatenate([right, gap, left, rest], axis=0).T[0:high]
-    lane = lax.broadcasted_iota(jnp.int32, (high, LANE), 1)
-    ghost = (lane < DEPTH) | ((lane >= start) & (lane < LEFT))
-    for f, (ref, strip) in enumerate(((d_s, strip_x), (out_r_ref, strip_r), (c_s, strip_c))):
-        side = pltpu.roll(sides, LANE - f * DEPTH, 1) if f else sides
-        ref[...] = jnp.where(ghost, side, strip[...])
+    lane = lax.broadcasted_iota(jnp.int32, (SUB, LANE), 1)
+    ghost = ((lane >= start) & (lane < LEFT)) | (lane < DEPTH)
+    fields = ((d_s, strip_x), (out_r_ref, strip_r), (c_s, strip_c))
+    for t in range(high // SUB):
+        row, at = place(t)
+        rows = slice(t * SUB, (t + 1) * SUB)
+        both = jnp.where((lane >= at) & (lane < at + COLUMNS), right[row : row + SUB], left[row : row + SUB])
+        for f, (ref, strip) in enumerate(fields):
+            by = (LANE - at - f * DEPTH) % LANE
+            ref[rows, :] = jnp.where(ghost, pltpu.roll(both, by, 1) if by else both, strip[rows, :])
     lane = lax.broadcasted_iota(jnp.int32, (SUB, LANE), 1)
     weigh = ((lane >= LEFT) & (lane < LEFT + SUB)) | (lane >= LANE - SUB)
-    ends = sweeps(out_x_ref.shape[0] // SUB, out_x_ref, d_s, out_r_ref, c_s, weigh)
+    ends = staggered(out_x_ref.shape[0] // SUB, out_x_ref, d_s, out_r_ref, c_s, weigh, 3)
     upper, lower = settled(pair_add(ends, (pair_ref[0:SUB, :], pair_ref[SUB : 2 * SUB, :])))
     tile = jnp.where(lane < LANE // 2, upper, lower)
     for i in range(pairs_ref.shape[0] // SUB):
@@ -304,7 +349,7 @@
         upper = pairs_ref[i * SUB : (i + 1) * SUB, :]
         pairs.append((upper, pltpu.roll(upper, LANE // 2, 1)))
     upper, lower = settled(pair_total(pairs))
-    norm_s[0] = jnp.sqrt((upper + lower) * (1.0 / cells))[0, 0]
+    norm_s[...] = jnp.sqrt((upper + lower) * (1.0 / cells))[0, 0:1]
     copies.append(pltpu.make_async_copy(norm_s, norm_hbm, sem.at[2]))
     copies[2].start()
     for copy in copies:
@@ -328,11 +373,10 @@
     devices = wide * high
     assert rows % SUB == 0 and cols % LANE == 0 and devices % SUB == 0
     assert wide % 2 == 0 and high % 2 == 0
-    assert rows % LANE + 2 * SUB <= LANE // 2 and FIELDS * DEPTH <= COLUMNS
+    assert FIELDS * DEPTH <= COLUMNS
     n = FIELDS * SUB
     tall = rows + 2 * SUB
-    span = rows // LANE * LANE + LANE
-    packed = span // LANE * COLUMNS - SUB
+    packed = -(-tall // (SUB * (LANE // COLUMNS))) * SUB
     f32 = functools.partial(jax.ShapeDtypeStruct, dtype=jnp.float32)
     held = functools.partial(pltpu.VMEM, dtype=jnp.float32)
     fields = [pltpu.with_memory_space_constraint(v, pltpu.HBM) for v in (forcing, guess, shift, ocean)]
@@ -350,7 +394,7 @@
 
     def next_chip(b, j):
         if j == 0:
-            return (b ^ 1, j)
+            return (wide - 1 - b, j)
         if j == high - 1:
             return (wide - 1 - b, j)
         return (b, ((j - 1) ^ 1) + 1)
@@ -366,7 +410,7 @@
     near = swap(near, shape, own_chip)
     x, f, c, columns = call(
         block_kernel,
-        (f32((rows, cols)),) * 3 + (f32((2 * COLUMNS, span)),),
+        (f32((rows, cols)),) * 3 + (f32((2 * packed, LANE)),),
         [HBM] * 4,
         (VMEM,) * 4,
         [pltpu.VMEM((rows, cols), v.dtype) for v in fields] + [pltpu.SemaphoreType.DMA((4,))],
@@ -400,7 +444,7 @@
         (f32((rows, cols)), f32((rows, cols)), f32((1,))),
         [VMEM] * 5,
         (HBM,) * 3,
-        [pltpu.VMEM((rows, cols), jnp.float32)] * 2 + [pltpu.SMEM((1,), jnp.float32), pltpu.SemaphoreType.DMA((3,))],
+        [pltpu.VMEM((rows, cols), jnp.float32)] * 2 + [pltpu.VMEM((1,), jnp.float32), pltpu.SemaphoreType.DMA((3,))],
     )(pairs, x, r, strip_x, strip_r)
     return (x, r, norm[0])
 

time: 26 us -> 25.8 us (level)
  blocking collectives: 10.7 us -> 9.81 us
  starting transfers between devices: 6.76 us -> 7.51 us
    all_to_all x1, blocking collectives: 10.7 us -> 9.81 us  [per_device(): pairs = lax.all_to_all(pairs, ('bx', 'by'), 0, 0, tiled=True)]
    ppermute x4, starting transfers between devices: 6.76 us -> 7.51 us  [swap(): return lax.ppermute(value, ('bx', 'by'), moves)]
where the time goes in v7:
time: 25.8 us; the launch traced here: 25.5 us
  blocking collectives  9.81 us (38%)
  starting transfers between devices  7.51 us (29%)
  Pallas kernels  5.7 us (22%)
  waiting for transfers between devices  1.87 us (7%)
  between operations  0.66 us (3%)
    all_to_all x1, blocking collectives, per_device(): pairs = lax.all_to_all(pairs, ('bx', 'by'), 0, 0, tiled=True)  9.81 us
    ppermute x4, starting transfers between devices, swap(): return lax.ppermute(value, ('bx', 'by'), moves)  7.51 us
    ppermute x4, waiting for transfers between devices, swap(): return lax.ppermute(value, ('bx', 'by'), moves)  1.87 us
    pallas_call x1, Pallas kernels, per_device(): call(interior_kernel, (held((rows, cols)), held((tall, cols)), held((2 *...  1.71 us
    pallas_call x1, Pallas kernels, per_device(): call(block_kernel, (f32((rows, cols)),) * 3 + (f32((2 * packed, LANE)),),...  1.37 us
    pallas_call x1, Pallas kernels, per_device(): call(edge_kernel, (f32((n, cols)),) * 2, [HBM] * 4, (VMEM,) * 2, edges *...  0.89 us
    pallas_call x1, Pallas kernels, per_device(): call(functools.partial(norm_kernel, rows * cols * devices), (f32((rows, c...  0.84 us
    pallas_call x1, Pallas kernels, per_device(): call(strip_kernel, (held((rows, LANE)), held(high), held((devices, LANE))...  0.79 us
  transfers between devices with their start and end apart: 4, of which 2 were waited for; matrix products, arithmetic and copies ran while one was open for 0% of the time, Pallas kernels for 12%

profile of v7, /device:TPU:0, one launch (start us, length us, event | category | flops | bytes accessed | tf_op | source)
XLA Modules:
  0.0 25.5 jit_solution(9584791361066281760)
XLA Ops:
  0.6 0.9 %shard_map.68 = (f32[24,256]{1,0:T(8,128)S(1)}, f32[24,256]{1,0:T(8,128)S(1)}) custom-call(f32[152,256]{1,0:T(8,128)} %refs_0_.3, f32[152,256]{1,0:T(8,128)} %refs_1_.3, f32[152,256]{1,0:T(8,128)} %refs_2_.3, s32[152,256]{1,0:T(8,128)} %refs_3_.3), custom_call_target="tpu_custom_call" | custom-call | flops 100000 | tf_op jit(solution)/shard_map/pallas_call | solution.py:384
  1.5 4.0 %collective-permute-start = (f32[24,256]{1,0:T(8,128)S(1)}, f32[24,256]{1,0:T(8,128)S(1)}, u32[]{:S(2)}, u32[]{:S(2)}) collective-permute-start(f32[24,256]{1,0:T(8,128)S(1)} %get-tuple-element.27), channel_id=1, source_target_pairs={{0,24},{1,2},{2,1},{3,4},{4,3},{5,6},{6,5},{7,31},{8,16},{9,10},{1... | collective-permute-start | bytes 73736 | tf_op jit(solution)/shard_map/ppermute | solution.py:367
  5.5 0.0 collective-permute-start.1
  5.5 1.4 %shard_map.67 = (f32[152,256]{1,0:T(8,128)S(1)}, f32[152,256]{1,0:T(8,128)S(1)}, f32[152,256]{1,0:T(8,128)S(1)}, f32[48,128]{1,0:T(8,128)S(1)}) custom-call(f32[152,256]{1,0:T(8,128)} %refs_0_.3, f32[152,256]{1,0:T(8,128)} %refs_1_.3, f32[152,256]{1,0:T(8,128)} %refs_2_.3, s32[152,256]{1,0:T(8,128)} %refs_3_.3), custom_call_target="tpu_custom_call" | custom-call | flops 100000 | tf_op jit(solution)/shard_map/pallas_call | solution.py:411
  6.9 0.4 %collective-permute-done.far_ref = f32[24,256]{1,0:T(8,128)S(1)} collective-permute-done((f32[24,256]{1,0:T(8,128)S(1)}, f32[24,256]{1,0:T(8,128)S(1)}, u32[]{:S(2)}, u32[]{:S(2)}) %collective-permute-start) | collective-permute-done | bytes 24608 | tf_op jit(solution)/shard_map/ppermute | solution.py:367
  7.3 0.0 collective-permute-done.1.near_ref
  7.3 0.1 shard_map.69
  7.4 3.0 %collective-permute-start.2 = (f32[24,128]{1,0:T(8,128)S(1)}, f32[24,128]{1,0:T(8,128)S(1)}, u32[]{:S(2)}, u32[]{:S(2)}) collective-permute-start(f32[24,128]{1,0:T(8,128)S(1)} %get-tuple-element.34), channel_id=1, source_target_pairs={{0,24},{1,25},{2,26},{3,27},{4,28},{5,29},{6,30},{7,31},{8,16},{9,... | collective-permute-start | bytes 36872 | tf_op jit(solution)/shard_map/ppermute | solution.py:367
  10.4 0.5 %collective-permute-start.3 = (f32[24,128]{1,0:T(8,128)S(1)}, f32[24,128]{1,0:T(8,128)S(1)}, u32[]{:S(2)}, u32[]{:S(2)}) collective-permute-start(f32[24,128]{1,0:T(8,128)S(1)} %get-tuple-element.35), channel_id=1, source_target_pairs={{0,8},{1,9},{2,10},{3,11},{4,12},{5,13},{6,14},{7,15},{8,0},{9,1},... | collective-permute-start | bytes 36872 | tf_op jit(solution)/shard_map/ppermute | solution.py:367
  10.9 1.7 %shard_map.70 = (f32[152,256]{1,0:T(8,128)S(1)}, f32[168,256]{1,0:T(8,128)S(1)}, f32[16,128]{1,0:T(8,128)S(1)}, f32[168,128]{1,0:T(8,128)S(1)}, f32[168,128]{1,0:T(8,128)S(1)}, /*index=5*/f32[168,128]{1,0:T(8,128)S(1)}) custom-call(f32[152,256]{1,0:T(8,128)S(1)} %get-tuple-element.24.x_ref, f32[152,256]{1,0:T(8,128)S(1)} %get-tuple-element.25.f_ref, ...), custom_call_target="tpu_custom_call" | custom-call | flops 100000 | tf_op jit(solution)/shard_map/pallas_call | solution.py:427
  12.7 0.0 collective-permute-done.2.b_ref
  12.7 1.4 %collective-permute-done.3.a_ref = f32[24,128]{1,0:T(8,128)S(1)} collective-permute-done((f32[24,128]{1,0:T(8,128)S(1)}, f32[24,128]{1,0:T(8,128)S(1)}, u32[]{:S(2)}, u32[]{:S(2)}) %collective-permute-start.3) | collective-permute-done | bytes 12320 | tf_op jit(solution)/shard_map/ppermute | solution.py:367
  14.1 0.8 %shard_map.71 = (f32[152,128]{1,0:T(8,128)S(1)}, f32[168,128]{1,0:T(8,128)S(1)}, f32[32,128]{1,0:T(8,128)S(1)}) custom-call(f32[168,128]{1,0:T(8,128)S(1)} %get-tuple-element.31.strip_x, f32[168,128]{1,0:T(8,128)S(1)} %get-tuple-element.32.strip_r, f32[168,128]{1,0:T(8,128)S(1)} %get-tuple-element.33.strip_c, f32[24,128]{1,0:T(8,128)S(1)} %collective-permute-done.2.b_ref, ...), custom_call_target="tpu_custom_call" | custom-call | flops 100000 | tf_op jit(solution)/shard_map/pallas_call | solution.py:434
  14.9 9.8 %all_to_all.11 = f32[32,1,128]{2,1,0:T(1,128)S(1)} all-to-all(f32[32,1,128]{2,1,0:T(1,128)S(1)} %bitcast.6), channel_id=1, replica_groups=mesh['bx'=4,'by'=8] {'bx','by'}, dimensions={0} | all-to-all | bytes 32768 | tf_op jit(solution)/shard_map/all_to_all | solution.py:441
  24.7 0.8 %shard_map.72 = (f32[152,256]{1,0:T(8,128)}, f32[152,256]{1,0:T(8,128)}, f32[1]{0:T(128)}) custom-call(f32[32,128]{1,0:T(8,128)S(1)} %bitcast.5, f32[152,256]{1,0:T(8,128)S(1)} %get-tuple-element.38.x_ref, f32[168,256]{1,0:T(8,128)S(1)} %get-tuple-element.39.r_ref, f32[152,128]{1,0:T(8,128)S(1)} %get-tuple-element.40.strip_x, ...), custom_call_target="tpu_custom_call" | custom-call | flops 100000 | tf_op jit(solution)/shard_map/pallas_call | solution.py:442
Async XLA Ops:
  1.5 5.8 %collective-permute-start = (f32[24,256]{1,0:T(8,128)S(1)}, f32[24,256]{1,0:T(8,128)S(1)}, u32[]{:S(2)}, u32[]{:S(2)}) collective-permute-start(f32[24,256]{1,0:T(8,128)S(1)} %get-tuple-element.27), channel_id=1, source_target_pairs={{0,24},{1,2},{2,1},{3,4},{4,3},{5,6},{6,5},{7,31},{8,16},{9,10},{1... | collective-permute-start | bytes 73736 | tf_op jit(solution)/shard_map/ppermute | solution.py:367
  5.5 1.8 %collective-permute-start.1 = (f32[24,256]{1,0:T(8,128)S(1)}, f32[24,256]{1,0:T(8,128)S(1)}, u32[]{:S(2)}, u32[]{:S(2)}) collective-permute-start(f32[24,256]{1,0:T(8,128)S(1)} %get-tuple-element.28), channel_id=1, source_target_pairs={{0,1},{1,0},{2,3},{3,2},{4,5},{5,4},{6,7},{7,6},{8,9},{9,8},{10,11... | collective-permute-start | bytes 73736 | tf_op jit(solution)/shard_map/ppermute | solution.py:367
  7.4 5.2 %collective-permute-start.2 = (f32[24,128]{1,0:T(8,128)S(1)}, f32[24,128]{1,0:T(8,128)S(1)}, u32[]{:S(2)}, u32[]{:S(2)}) collective-permute-start(f32[24,128]{1,0:T(8,128)S(1)} %get-tuple-element.34), channel_id=1, source_target_pairs={{0,24},{1,25},{2,26},{3,27},{4,28},{5,29},{6,30},{7,31},{8,16},{9,... | collective-permute-start | bytes 36872 | tf_op jit(solution)/shard_map/ppermute | solution.py:367
  10.4 3.7 %collective-permute-start.3 = (f32[24,128]{1,0:T(8,128)S(1)}, f32[24,128]{1,0:T(8,128)S(1)}, u32[]{:S(2)}, u32[]{:S(2)}) collective-permute-start(f32[24,128]{1,0:T(8,128)S(1)} %get-tuple-element.35), channel_id=1, source_target_pairs={{0,8},{1,9},{2,10},{3,11},{4,12},{5,13},{6,14},{7,15},{8,0},{9,1},... | collective-permute-start | bytes 36872 | tf_op jit(solution)/shard_map/ppermute | solution.py:367

commit v8 on v7

--- a/solution.py
+++ b/solution.py
@@ -238,8 +238,8 @@
     return pair_total([(q, zero) for q in squares])
 
 
-def staggered(inner, x_s, d_s, r_s, c_s, weigh, lag):
-    tall, wide = d_s.shape
+def staggered(inner, fill, x_s, r_s, c_s, weigh, lag):
+    tall, wide = c_s.shape
     tiles = tall // SUB
     theta, steps = coefficients()
     row_id = lax.broadcasted_iota(jnp.int32, (SUB, wide), 0)
@@ -255,8 +255,7 @@
     held = [{} for _ in range(ITERS + 1)]
     for step in range(tiles + 1 + lag * ITERS):
         if step < tiles:
-            at = order[step] * SUB
-            held[0][step] = across(d_s[at : at + SUB, :])
+            held[0][step] = across(fill(order[step]))
         for sweep in range(ITERS + 1):
             p = step - 1 - lag * sweep
             if not 0 <= p < tiles:
@@ -308,25 +307,28 @@
     pair_ref[SUB : 2 * SUB, :] = jnp.broadcast_to(lower, (SUB, LANE))
 
 
-def strip_kernel(strip_x, strip_r, strip_c, b_ref, a_ref, pair_ref, out_x_ref, out_r_ref, pairs_ref, d_s, c_s):
+def strip_kernel(strip_x, strip_r, strip_c, b_ref, a_ref, pair_ref, out_x_ref, out_r_ref, pairs_ref, c_s):
     odd_x = is_odd("bx")
-    high = d_s.shape[0]
     a, b = a_ref[...], b_ref[...]
     left, right = jnp.where(odd_x, a, b), jnp.where(odd_x, b, a)
     start = LEFT - DEPTH
     lane = lax.broadcasted_iota(jnp.int32, (SUB, LANE), 1)
     ghost = ((lane >= start) & (lane < LEFT)) | (lane < DEPTH)
-    fields = ((d_s, strip_x), (out_r_ref, strip_r), (c_s, strip_c))
-    for t in range(high // SUB):
+
+    def fill(t):
         row, at = place(t)
         rows = slice(t * SUB, (t + 1) * SUB)
         both = jnp.where((lane >= at) & (lane < at + COLUMNS), right[row : row + SUB], left[row : row + SUB])
-        for f, (ref, strip) in enumerate(fields):
+        values = []
+        for f, strip in enumerate((strip_x, strip_r, strip_c)):
             by = (LANE - at - f * DEPTH) % LANE
-            ref[rows, :] = jnp.where(ghost, pltpu.roll(both, by, 1) if by else both, strip[rows, :])
+            values.append(jnp.where(ghost, pltpu.roll(both, by, 1) if by else both, strip[rows, :]))
+        out_r_ref[rows, :], c_s[rows, :] = values[1:]
+        return values[0]
+
     lane = lax.broadcasted_iota(jnp.int32, (SUB, LANE), 1)
     weigh = ((lane >= LEFT) & (lane < LEFT + SUB)) | (lane >= LANE - SUB)
-    ends = staggered(out_x_ref.shape[0] // SUB, out_x_ref, d_s, out_r_ref, c_s, weigh, 3)
+    ends = staggered(out_x_ref.shape[0] // SUB, fill, out_x_ref, out_r_ref, c_s, weigh, 3)
     upper, lower = settled(pair_add(ends, (pair_ref[0:SUB, :], pair_ref[SUB : 2 * SUB, :])))
     tile = jnp.where(lane < LANE // 2, upper, lower)
     for i in range(pairs_ref.shape[0] // SUB):
@@ -436,7 +438,7 @@
         (held((rows, LANE)), held(high), held((devices, LANE))),
         [VMEM] * 6,
         (VMEM,) * 3,
-        [pltpu.VMEM(high, jnp.float32)] * 2,
+        [pltpu.VMEM(high, jnp.float32)],
     )(*strips, b, a, pair)
     pairs = lax.all_to_all(pairs, ("bx", "by"), 0, 0, tiled=True)
     x, r, norm = call(

time: 25.8 us -> 25.8 us (level)
  no operation moved by 1% of the time
where the time goes in v8:
time: 25.8 us; the launch traced here: 25.5 us
  blocking collectives  9.81 us (38%)
  starting transfers between devices  7.51 us (29%)
  Pallas kernels  5.66 us (22%)
  waiting for transfers between devices  1.87 us (7%)
  between operations  0.66 us (3%)
    all_to_all x1, blocking collectives, per_device(): pairs = lax.all_to_all(pairs, ('bx', 'by'), 0, 0, tiled=True)  9.81 us
    ppermute x4, starting transfers between devices, swap(): return lax.ppermute(value, ('bx', 'by'), moves)  7.51 us
    ppermute x4, waiting for transfers between devices, swap(): return lax.ppermute(value, ('bx', 'by'), moves)  1.87 us
    pallas_call x1, Pallas kernels, per_device(): call(interior_kernel, (held((rows, cols)), held((tall, cols)), held((2 *...  1.71 us
    pallas_call x1, Pallas kernels, per_device(): call(block_kernel, (f32((rows, cols)),) * 3 + (f32((2 * packed, LANE)),),...  1.37 us
    pallas_call x1, Pallas kernels, per_device(): call(edge_kernel, (f32((n, cols)),) * 2, [HBM] * 4, (VMEM,) * 2, edges *...  0.89 us
    pallas_call x1, Pallas kernels, per_device(): call(functools.partial(norm_kernel, rows * cols * devices), (f32((rows, c...  0.84 us
    pallas_call x1, Pallas kernels, per_device(): call(strip_kernel, (held((rows, LANE)), held(high), held((devices, LANE))...  0.75 us
  transfers between devices with their start and end apart: 4, of which 2 were waited for; matrix products, arithmetic and copies ran while one was open for 0% of the time, Pallas kernels for 12%

profile of v8, /device:TPU:0, one launch (start us, length us, event | category | flops | bytes accessed | tf_op | source)
XLA Modules:
  0.0 25.5 jit_solution(12146099014162102202)
XLA Ops:
  0.6 0.9 %shard_map.68 = (f32[24,256]{1,0:T(8,128)S(1)}, f32[24,256]{1,0:T(8,128)S(1)}) custom-call(f32[152,256]{1,0:T(8,128)} %refs_0_.3, f32[152,256]{1,0:T(8,128)} %refs_1_.3, f32[152,256]{1,0:T(8,128)} %refs_2_.3, s32[152,256]{1,0:T(8,128)} %refs_3_.3), custom_call_target="tpu_custom_call" | custom-call | flops 100000 | tf_op jit(solution)/shard_map/pallas_call | solution.py:386
  1.5 4.0 %collective-permute-start = (f32[24,256]{1,0:T(8,128)S(1)}, f32[24,256]{1,0:T(8,128)S(1)}, u32[]{:S(2)}, u32[]{:S(2)}) collective-permute-start(f32[24,256]{1,0:T(8,128)S(1)} %get-tuple-element.27), channel_id=1, source_target_pairs={{0,24},{1,2},{2,1},{3,4},{4,3},{5,6},{6,5},{7,31},{8,16},{9,10},{1... | collective-permute-start | bytes 73736 | tf_op jit(solution)/shard_map/ppermute | solution.py:369
  5.5 0.0 collective-permute-start.1
  5.5 1.4 %shard_map.67 = (f32[152,256]{1,0:T(8,128)S(1)}, f32[152,256]{1,0:T(8,128)S(1)}, f32[152,256]{1,0:T(8,128)S(1)}, f32[48,128]{1,0:T(8,128)S(1)}) custom-call(f32[152,256]{1,0:T(8,128)} %refs_0_.3, f32[152,256]{1,0:T(8,128)} %refs_1_.3, f32[152,256]{1,0:T(8,128)} %refs_2_.3, s32[152,256]{1,0:T(8,128)} %refs_3_.3), custom_call_target="tpu_custom_call" | custom-call | flops 100000 | tf_op jit(solution)/shard_map/pallas_call | solution.py:413
  6.9 0.4 %collective-permute-done.far_ref = f32[24,256]{1,0:T(8,128)S(1)} collective-permute-done((f32[24,256]{1,0:T(8,128)S(1)}, f32[24,256]{1,0:T(8,128)S(1)}, u32[]{:S(2)}, u32[]{:S(2)}) %collective-permute-start) | collective-permute-done | bytes 24608 | tf_op jit(solution)/shard_map/ppermute | solution.py:369
  7.3 0.0 collective-permute-done.1.near_ref
  7.3 0.1 shard_map.69
  7.4 3.0 %collective-permute-start.2 = (f32[24,128]{1,0:T(8,128)S(1)}, f32[24,128]{1,0:T(8,128)S(1)}, u32[]{:S(2)}, u32[]{:S(2)}) collective-permute-start(f32[24,128]{1,0:T(8,128)S(1)} %get-tuple-element.34), channel_id=1, source_target_pairs={{0,24},{1,25},{2,26},{3,27},{4,28},{5,29},{6,30},{7,31},{8,16},{9,... | collective-permute-start | bytes 36872 | tf_op jit(solution)/shard_map/ppermute | solution.py:369
  10.4 0.5 %collective-permute-start.3 = (f32[24,128]{1,0:T(8,128)S(1)}, f32[24,128]{1,0:T(8,128)S(1)}, u32[]{:S(2)}, u32[]{:S(2)}) collective-permute-start(f32[24,128]{1,0:T(8,128)S(1)} %get-tuple-element.35), channel_id=1, source_target_pairs={{0,8},{1,9},{2,10},{3,11},{4,12},{5,13},{6,14},{7,15},{8,0},{9,1},... | collective-permute-start | bytes 36872 | tf_op jit(solution)/shard_map/ppermute | solution.py:369
  10.9 1.7 %shard_map.70 = (f32[152,256]{1,0:T(8,128)S(1)}, f32[168,256]{1,0:T(8,128)S(1)}, f32[16,128]{1,0:T(8,128)S(1)}, f32[168,128]{1,0:T(8,128)S(1)}, f32[168,128]{1,0:T(8,128)S(1)}, /*index=5*/f32[168,128]{1,0:T(8,128)S(1)}) custom-call(f32[152,256]{1,0:T(8,128)S(1)} %get-tuple-element.24.x_ref, f32[152,256]{1,0:T(8,128)S(1)} %get-tuple-element.25.f_ref, ...), custom_call_target="tpu_custom_call" | custom-call | flops 100000 | tf_op jit(solution)/shard_map/pallas_call | solution.py:429
  12.7 0.0 collective-permute-done.2.b_ref
  12.7 1.4 %collective-permute-done.3.a_ref = f32[24,128]{1,0:T(8,128)S(1)} collective-permute-done((f32[24,128]{1,0:T(8,128)S(1)}, f32[24,128]{1,0:T(8,128)S(1)}, u32[]{:S(2)}, u32[]{:S(2)}) %collective-permute-start.3) | collective-permute-done | bytes 12320 | tf_op jit(solution)/shard_map/ppermute | solution.py:369
  14.1 0.8 %shard_map.71 = (f32[152,128]{1,0:T(8,128)S(1)}, f32[168,128]{1,0:T(8,128)S(1)}, f32[32,128]{1,0:T(8,128)S(1)}) custom-call(f32[168,128]{1,0:T(8,128)S(1)} %get-tuple-element.31.strip_x, f32[168,128]{1,0:T(8,128)S(1)} %get-tuple-element.32.strip_r, f32[168,128]{1,0:T(8,128)S(1)} %get-tuple-element.33.strip_c, f32[24,128]{1,0:T(8,128)S(1)} %collective-permute-done.2.b_ref, ...), custom_call_target="tpu_custom_call" | custom-call | flops 100000 | tf_op jit(solution)/shard_map/pallas_call | solution.py:436
  14.9 9.8 %all_to_all.11 = f32[32,1,128]{2,1,0:T(1,128)S(1)} all-to-all(f32[32,1,128]{2,1,0:T(1,128)S(1)} %bitcast.6), channel_id=1, replica_groups=mesh['bx'=4,'by'=8] {'bx','by'}, dimensions={0} | all-to-all | bytes 32768 | tf_op jit(solution)/shard_map/all_to_all | solution.py:443
  24.7 0.8 %shard_map.72 = (f32[152,256]{1,0:T(8,128)}, f32[152,256]{1,0:T(8,128)}, f32[1]{0:T(128)}) custom-call(f32[32,128]{1,0:T(8,128)S(1)} %bitcast.5, f32[152,256]{1,0:T(8,128)S(1)} %get-tuple-element.38.x_ref, f32[168,256]{1,0:T(8,128)S(1)} %get-tuple-element.39.r_ref, f32[152,128]{1,0:T(8,128)S(1)} %get-tuple-element.40.strip_x, ...), custom_call_target="tpu_custom_call" | custom-call | flops 100000 | tf_op jit(solution)/shard_map/pallas_call | solution.py:444
Async XLA Ops:
  1.5 5.8 %collective-permute-start = (f32[24,256]{1,0:T(8,128)S(1)}, f32[24,256]{1,0:T(8,128)S(1)}, u32[]{:S(2)}, u32[]{:S(2)}) collective-permute-start(f32[24,256]{1,0:T(8,128)S(1)} %get-tuple-element.27), channel_id=1, source_target_pairs={{0,24},{1,2},{2,1},{3,4},{4,3},{5,6},{6,5},{7,31},{8,16},{9,10},{1... | collective-permute-start | bytes 73736 | tf_op jit(solution)/shard_map/ppermute | solution.py:369
  5.5 1.8 %collective-permute-start.1 = (f32[24,256]{1,0:T(8,128)S(1)}, f32[24,256]{1,0:T(8,128)S(1)}, u32[]{:S(2)}, u32[]{:S(2)}) collective-permute-start(f32[24,256]{1,0:T(8,128)S(1)} %get-tuple-element.28), channel_id=1, source_target_pairs={{0,1},{1,0},{2,3},{3,2},{4,5},{5,4},{6,7},{7,6},{8,9},{9,8},{10,11... | collective-permute-start | bytes 73736 | tf_op jit(solution)/shard_map/ppermute | solution.py:369
  7.4 5.2 %collective-permute-start.2 = (f32[24,128]{1,0:T(8,128)S(1)}, f32[24,128]{1,0:T(8,128)S(1)}, u32[]{:S(2)}, u32[]{:S(2)}) collective-permute-start(f32[24,128]{1,0:T(8,128)S(1)} %get-tuple-element.34), channel_id=1, source_target_pairs={{0,24},{1,25},{2,26},{3,27},{4,28},{5,29},{6,30},{7,31},{8,16},{9,... | collective-permute-start | bytes 36872 | tf_op jit(solution)/shard_map/ppermute | solution.py:369
  10.4 3.7 %collective-permute-start.3 = (f32[24,128]{1,0:T(8,128)S(1)}, f32[24,128]{1,0:T(8,128)S(1)}, u32[]{:S(2)}, u32[]{:S(2)}) collective-permute-start(f32[24,128]{1,0:T(8,128)S(1)} %get-tuple-element.35), channel_id=1, source_target_pairs={{0,8},{1,9},{2,10},{3,11},{4,12},{5,13},{6,14},{7,15},{8,0},{9,1},... | collective-permute-start | bytes 36872 | tf_op jit(solution)/shard_map/ppermute | solution.py:369

commit v9 on v8

--- a/solution.py
+++ b/solution.py
@@ -53,21 +53,20 @@
     low_s, top_s = refs[6:10], refs[10:14]
     sem = refs[14]
     rows = refs[0].shape[0]
+    odd = is_odd("by")
+    first = pl.multiple_of(jnp.where(odd, 0, rows - SUB), SUB)
+    second = pl.multiple_of(jnp.where(odd, rows - SUB, 0), SUB)
     copies = []
     for i in range(4):
-        copies.append(pltpu.make_async_copy(refs[i].at[0:SUB, :], low_s[i], sem.at[2 * i]))
-        copies.append(pltpu.make_async_copy(refs[i].at[rows - SUB : rows, :], top_s[i], sem.at[2 * i + 1]))
+        copies.append(pltpu.make_async_copy(refs[i].at[pl.ds(second, SUB), :], top_s[i], sem.at[2 * i + 1]))
+        copies.append(pltpu.make_async_copy(refs[i].at[pl.ds(first, SUB), :], low_s[i], sem.at[2 * i]))
     for copy in copies:
         copy.start()
-    odd = is_odd("by")
     for copy in copies:
         copy.wait()
-    low = masked_fields(*(ref[...] for ref in low_s))
-    top = masked_fields(*(ref[...] for ref in top_s))
-    for f in range(FIELDS):
-        at = slice(f * SUB, (f + 1) * SUB)
-        near_ref[at, :] = jnp.where(odd, low[f], top[f])
-        far_ref[at, :] = jnp.where(odd, top[f], low[f])
+    for out, held in ((near_ref, low_s), (far_ref, top_s)):
+        for f, field in enumerate(masked_fields(*(ref[...] for ref in held))):
+            out[f * SUB : (f + 1) * SUB, :] = field
 
 
 def place(index):

time: 25.8 us -> 25.8 us (level)
  no operation moved by 1% of the time
where the time goes in v9:
time: 25.8 us; the launch traced here: 25.5 us
  blocking collectives  9.81 us (38%)
  starting transfers between devices  7.51 us (29%)
  Pallas kernels  5.67 us (22%)
  waiting for transfers between devices  1.87 us (7%)
  between operations  0.66 us (3%)
    all_to_all x1, blocking collectives, per_device(): pairs = lax.all_to_all(pairs, ('bx', 'by'), 0, 0, tiled=True)  9.81 us
    ppermute x4, starting transfers between devices, swap(): return lax.ppermute(value, ('bx', 'by'), moves)  7.51 us
    ppermute x4, waiting for transfers between devices, swap(): return lax.ppermute(value, ('bx', 'by'), moves)  1.87 us
    pallas_call x1, Pallas kernels, per_device(): call(interior_kernel, (held((rows, cols)), held((tall, cols)), held((2 *...  1.71 us
    pallas_call x1, Pallas kernels, per_device(): call(block_kernel, (f32((rows, cols)),) * 3 + (f32((2 * packed, LANE)),),...  1.37 us
    pallas_call x1, Pallas kernels, per_device(): call(edge_kernel, (f32((n, cols)),) * 2, [HBM] * 4, (VMEM,) * 2, edges *...  0.9 us
    pallas_call x1, Pallas kernels, per_device(): call(functools.partial(norm_kernel, rows * cols * devices), (f32((rows, c...  0.84 us
    pallas_call x1, Pallas kernels, per_device(): call(strip_kernel, (held((rows, LANE)), held(high), held((devices, LANE))...  0.75 us
  transfers between devices with their start and end apart: 4, of which 2 were waited for; matrix products, arithmetic and copies ran while one was open for 0% of the time, Pallas kernels for 12%

profile of v9, /device:TPU:0, one launch (start us, length us, event | category | flops | bytes accessed | tf_op | source)
XLA Modules:
  0.0 25.5 jit_solution(3996575185287805255)
XLA Ops:
  0.6 0.9 %shard_map.68 = (f32[24,256]{1,0:T(8,128)S(1)}, f32[24,256]{1,0:T(8,128)S(1)}) custom-call(f32[152,256]{1,0:T(8,128)} %refs_0_.3, f32[152,256]{1,0:T(8,128)} %refs_1_.3, f32[152,256]{1,0:T(8,128)} %refs_2_.3, s32[152,256]{1,0:T(8,128)} %refs_3_.3), custom_call_target="tpu_custom_call" | custom-call | flops 100000 | tf_op jit(solution)/shard_map/pallas_call | solution.py:385
  1.5 4.0 %collective-permute-start = (f32[24,256]{1,0:T(8,128)S(1)}, f32[24,256]{1,0:T(8,128)S(1)}, u32[]{:S(2)}, u32[]{:S(2)}) collective-permute-start(f32[24,256]{1,0:T(8,128)S(1)} %get-tuple-element.27), channel_id=1, source_target_pairs={{0,24},{1,2},{2,1},{3,4},{4,3},{5,6},{6,5},{7,31},{8,16},{9,10},{1... | collective-permute-start | bytes 73736 | tf_op jit(solution)/shard_map/ppermute | solution.py:368
  5.5 0.0 collective-permute-start.1
  5.5 1.4 %shard_map.67 = (f32[152,256]{1,0:T(8,128)S(1)}, f32[152,256]{1,0:T(8,128)S(1)}, f32[152,256]{1,0:T(8,128)S(1)}, f32[48,128]{1,0:T(8,128)S(1)}) custom-call(f32[152,256]{1,0:T(8,128)} %refs_0_.3, f32[152,256]{1,0:T(8,128)} %refs_1_.3, f32[152,256]{1,0:T(8,128)} %refs_2_.3, s32[152,256]{1,0:T(8,128)} %refs_3_.3), custom_call_target="tpu_custom_call" | custom-call | flops 100000 | tf_op jit(solution)/shard_map/pallas_call | solution.py:412
  6.9 0.4 %collective-permute-done.far_ref = f32[24,256]{1,0:T(8,128)S(1)} collective-permute-done((f32[24,256]{1,0:T(8,128)S(1)}, f32[24,256]{1,0:T(8,128)S(1)}, u32[]{:S(2)}, u32[]{:S(2)}) %collective-permute-start) | collective-permute-done | bytes 24608 | tf_op jit(solution)/shard_map/ppermute | solution.py:368
  7.3 0.0 collective-permute-done.1.near_ref
  7.3 0.1 shard_map.69
  7.4 3.0 %collective-permute-start.2 = (f32[24,128]{1,0:T(8,128)S(1)}, f32[24,128]{1,0:T(8,128)S(1)}, u32[]{:S(2)}, u32[]{:S(2)}) collective-permute-start(f32[24,128]{1,0:T(8,128)S(1)} %get-tuple-element.34), channel_id=1, source_target_pairs={{0,24},{1,25},{2,26},{3,27},{4,28},{5,29},{6,30},{7,31},{8,16},{9,... | collective-permute-start | bytes 36872 | tf_op jit(solution)/shard_map/ppermute | solution.py:368
  10.4 0.5 %collective-permute-start.3 = (f32[24,128]{1,0:T(8,128)S(1)}, f32[24,128]{1,0:T(8,128)S(1)}, u32[]{:S(2)}, u32[]{:S(2)}) collective-permute-start(f32[24,128]{1,0:T(8,128)S(1)} %get-tuple-element.35), channel_id=1, source_target_pairs={{0,8},{1,9},{2,10},{3,11},{4,12},{5,13},{6,14},{7,15},{8,0},{9,1},... | collective-permute-start | bytes 36872 | tf_op jit(solution)/shard_map/ppermute | solution.py:368
  11.0 1.7 %shard_map.70 = (f32[152,256]{1,0:T(8,128)S(1)}, f32[168,256]{1,0:T(8,128)S(1)}, f32[16,128]{1,0:T(8,128)S(1)}, f32[168,128]{1,0:T(8,128)S(1)}, f32[168,128]{1,0:T(8,128)S(1)}, /*index=5*/f32[168,128]{1,0:T(8,128)S(1)}) custom-call(f32[152,256]{1,0:T(8,128)S(1)} %get-tuple-element.24.x_ref, f32[152,256]{1,0:T(8,128)S(1)} %get-tuple-element.25.f_ref, ...), custom_call_target="tpu_custom_call" | custom-call | flops 100000 | tf_op jit(solution)/shard_map/pallas_call | solution.py:428
  12.7 0.0 collective-permute-done.2.b_ref
  12.7 1.4 %collective-permute-done.3.a_ref = f32[24,128]{1,0:T(8,128)S(1)} collective-permute-done((f32[24,128]{1,0:T(8,128)S(1)}, f32[24,128]{1,0:T(8,128)S(1)}, u32[]{:S(2)}, u32[]{:S(2)}) %collective-permute-start.3) | collective-permute-done | bytes 12320 | tf_op jit(solution)/shard_map/ppermute | solution.py:368
  14.1 0.8 %shard_map.71 = (f32[152,128]{1,0:T(8,128)S(1)}, f32[168,128]{1,0:T(8,128)S(1)}, f32[32,128]{1,0:T(8,128)S(1)}) custom-call(f32[168,128]{1,0:T(8,128)S(1)} %get-tuple-element.31.strip_x, f32[168,128]{1,0:T(8,128)S(1)} %get-tuple-element.32.strip_r, f32[168,128]{1,0:T(8,128)S(1)} %get-tuple-element.33.strip_c, f32[24,128]{1,0:T(8,128)S(1)} %collective-permute-done.2.b_ref, ...), custom_call_target="tpu_custom_call" | custom-call | flops 100000 | tf_op jit(solution)/shard_map/pallas_call | solution.py:435
  14.9 9.8 %all_to_all.11 = f32[32,1,128]{2,1,0:T(1,128)S(1)} all-to-all(f32[32,1,128]{2,1,0:T(1,128)S(1)} %bitcast.6), channel_id=1, replica_groups=mesh['bx'=4,'by'=8] {'bx','by'}, dimensions={0} | all-to-all | bytes 32768 | tf_op jit(solution)/shard_map/all_to_all | solution.py:442
  24.7 0.8 %shard_map.72 = (f32[152,256]{1,0:T(8,128)}, f32[152,256]{1,0:T(8,128)}, f32[1]{0:T(128)}) custom-call(f32[32,128]{1,0:T(8,128)S(1)} %bitcast.5, f32[152,256]{1,0:T(8,128)S(1)} %get-tuple-element.38.x_ref, f32[168,256]{1,0:T(8,128)S(1)} %get-tuple-element.39.r_ref, f32[152,128]{1,0:T(8,128)S(1)} %get-tuple-element.40.strip_x, ...), custom_call_target="tpu_custom_call" | custom-call | flops 100000 | tf_op jit(solution)/shard_map/pallas_call | solution.py:443
Async XLA Ops:
  1.5 5.8 %collective-permute-start = (f32[24,256]{1,0:T(8,128)S(1)}, f32[24,256]{1,0:T(8,128)S(1)}, u32[]{:S(2)}, u32[]{:S(2)}) collective-permute-start(f32[24,256]{1,0:T(8,128)S(1)} %get-tuple-element.27), channel_id=1, source_target_pairs={{0,24},{1,2},{2,1},{3,4},{4,3},{5,6},{6,5},{7,31},{8,16},{9,10},{1... | collective-permute-start | bytes 73736 | tf_op jit(solution)/shard_map/ppermute | solution.py:368
  5.5 1.8 %collective-permute-start.1 = (f32[24,256]{1,0:T(8,128)S(1)}, f32[24,256]{1,0:T(8,128)S(1)}, u32[]{:S(2)}, u32[]{:S(2)}) collective-permute-start(f32[24,256]{1,0:T(8,128)S(1)} %get-tuple-element.28), channel_id=1, source_target_pairs={{0,1},{1,0},{2,3},{3,2},{4,5},{5,4},{6,7},{7,6},{8,9},{9,8},{10,11... | collective-permute-start | bytes 73736 | tf_op jit(solution)/shard_map/ppermute | solution.py:368
  7.4 5.2 %collective-permute-start.2 = (f32[24,128]{1,0:T(8,128)S(1)}, f32[24,128]{1,0:T(8,128)S(1)}, u32[]{:S(2)}, u32[]{:S(2)}) collective-permute-start(f32[24,128]{1,0:T(8,128)S(1)} %get-tuple-element.34), channel_id=1, source_target_pairs={{0,24},{1,25},{2,26},{3,27},{4,28},{5,29},{6,30},{7,31},{8,16},{9,... | collective-permute-start | bytes 36872 | tf_op jit(solution)/shard_map/ppermute | solution.py:368
  10.4 3.7 %collective-permute-start.3 = (f32[24,128]{1,0:T(8,128)S(1)}, f32[24,128]{1,0:T(8,128)S(1)}, u32[]{:S(2)}, u32[]{:S(2)}) collective-permute-start(f32[24,128]{1,0:T(8,128)S(1)} %get-tuple-element.35), channel_id=1, source_target_pairs={{0,8},{1,9},{2,10},{3,11},{4,12},{5,13},{6,14},{7,15},{8,0},{9,1},... | collective-permute-start | bytes 36872 | tf_op jit(solution)/shard_map/ppermute | solution.py:368
